TPU v7x, 16 devices: a whole 2x2x2 slice. The times are simulated.
16 devices in a mesh: emb: 16 (over z, y, x, core).
Axes of the slice: x: 2, y: 2, z: 2, core: 2. Of those that a mesh axis runs over, the one named last changes fastest.
Arguments:
- tok_ids: int32 [8192], P('emb')
- x_in: bfloat16 [8192, 1024], P('emb')
- d_out: bfloat16 [8192, 1024], P('emb')
- ple_tables: bfloat16 [4, 50304, 1024], P(None, 'emb')
- w_up: bfloat16 [4, 1024, 4096], replicated
- w_down: bfloat16 [4, 4096, 1024], replicated
- w_gate: bfloat16 [4, 1024, 1024], replicated
- w_proj: bfloat16 [4, 1024, 1024], replicated
Outputs:
- output 1: bfloat16 [8192, 1024], P('emb')
- output 2: float32 [4, 50304, 1024], P(None, 'emb')
- output 3: float32 [4, 1024, 4096], replicated
- output 4: float32 [4, 4096, 1024], replicated
- output 5: float32 [4, 1024, 1024], replicated
- output 6: float32 [4, 1024, 1024], replicated
All inputs are finite; a program needn't handle non-finite values.
Results may differ from a plain program's by a relative error of at most 0.0161681.
Values are sent between devices in bfloat16 or wider.
A program may use at most 1.25 GiB of HBM per device.

v0:
```python
import jax
import jax.numpy as jnp
from jax import lax
from jax.sharding import PartitionSpec as P

EPS = 1e-6
CAP_DIV = 4


def gelu_tanh(pre_act):
    return jax.nn.gelu(pre_act, approximate=True)


def gelu_back(pre_act, grad_out):
    _, pull_back = jax.vjp(gelu_tanh, pre_act.astype(jnp.float32))
    return pull_back(grad_out.astype(jnp.float32))[0]


def layer_fwd(x_cur, up_mat, down_mat, gate_mat, proj_mat, emb_rows):
    x_wide = x_cur.astype(jnp.float32)
    inv_rms = lax.rsqrt(jnp.mean(x_wide * x_wide, axis=-1, keepdims=True) + EPS)
    normed = (x_wide * inv_rms).astype(jnp.bfloat16)
    hidden = jnp.dot(normed, up_mat, preferred_element_type=jnp.float32).astype(jnp.bfloat16)
    act_out = gelu_tanh(hidden.astype(jnp.float32)).astype(jnp.bfloat16)
    mlp_out = jnp.dot(act_out, down_mat, preferred_element_type=jnp.float32).astype(jnp.bfloat16)
    gate_pre = jnp.dot(normed, gate_mat, preferred_element_type=jnp.float32).astype(jnp.bfloat16)
    gate_act = gelu_tanh(gate_pre.astype(jnp.float32)).astype(jnp.bfloat16)
    mix_rows = (gate_act.astype(jnp.float32) * emb_rows.astype(jnp.float32)).astype(jnp.bfloat16)
    ple_out = jnp.dot(mix_rows, proj_mat, preferred_element_type=jnp.float32).astype(jnp.bfloat16)
    x_next = (x_wide + mlp_out.astype(jnp.float32) + ple_out.astype(jnp.float32)).astype(jnp.bfloat16)
    return x_next, (x_wide, inv_rms, normed, hidden, act_out, gate_pre, gate_act, mix_rows)


def layer_bwd(d_x, saved, emb_rows, up_mat, down_mat, gate_mat, proj_mat):
    x_wide, inv_rms, normed, hidden, act_out, gate_pre, gate_act, mix_rows = saved
    g_out = d_x.astype(jnp.bfloat16)
    d_act = jnp.einsum("nd,fd->nf", g_out, down_mat, preferred_element_type=jnp.float32).astype(jnp.bfloat16)
    d_hidden = gelu_back(hidden, d_act).astype(jnp.bfloat16)
    d_mix = jnp.einsum("nd,ed->ne", g_out, proj_mat, preferred_element_type=jnp.float32).astype(jnp.bfloat16)
    d_rows = gate_act.astype(jnp.float32) * d_mix.astype(jnp.float32)
    d_gate_act = (emb_rows.astype(jnp.float32) * d_mix.astype(jnp.float32)).astype(jnp.bfloat16)
    d_gate_pre = gelu_back(gate_pre, d_gate_act).astype(jnp.bfloat16)
    d_norm = jnp.einsum("nf,df->nd", d_hidden, up_mat, preferred_element_type=jnp.float32) + jnp.einsum("ne,de->nd", d_gate_pre, gate_mat, preferred_element_type=jnp.float32)
    d_x_new = d_x + inv_rms * d_norm - inv_rms ** 3 * x_wide * jnp.mean(d_norm * x_wide, axis=-1, keepdims=True)
    g_up = jnp.einsum("nd,nf->df", normed, d_hidden, preferred_element_type=jnp.float32)
    g_down = jnp.einsum("nf,nd->fd", act_out, g_out, preferred_element_type=jnp.float32)
    g_gate = jnp.einsum("nd,ne->de", normed, d_gate_pre, preferred_element_type=jnp.float32)
    g_proj = jnp.einsum("ne,nd->ed", mix_rows, g_out, preferred_element_type=jnp.float32)
    return d_x_new, (g_up, g_down, g_gate, g_proj), d_rows


def solution(mesh):
    shards = mesh.shape["emb"]

    def device_step(tok_ids, x_in, d_out, ple_tables, w_up, w_down, w_gate, w_proj):
        layers = ple_tables.shape[0]
        rows_dev = ple_tables.shape[1]
        cap_rows = tok_ids.shape[0] // CAP_DIV
        owner_dev = tok_ids // rows_dev
        local_row = tok_ids - owner_dev * rows_dev
        owner_hot = (owner_dev[:, None] == jnp.arange(shards, dtype=jnp.int32)[None, :]).astype(jnp.int32)
        slot_rank = jnp.sum((jnp.cumsum(owner_hot, axis=0) - owner_hot) * owner_hot, axis=1)
        dest_slot = owner_dev * cap_rows + slot_rank
        req_send = jnp.zeros((shards * cap_rows,), jnp.int32).at[dest_slot].set(local_row)
        req_recv = lax.all_to_all(req_send, "emb", 0, 0, tiled=True)
        x_cur = x_in
        saved_list = []
        rows_list = []
        for layer_idx in range(layers):
            served = jnp.take(ple_tables[layer_idx], req_recv, axis=0)
            returned = lax.all_to_all(served, "emb", 0, 0, tiled=True)
            emb_rows = jnp.take(returned, dest_slot, axis=0)
            x_cur, saved = layer_fwd(x_cur, w_up[layer_idx], w_down[layer_idx], w_gate[layer_idx], w_proj[layer_idx], emb_rows)
            saved_list.append(saved)
            rows_list.append(emb_rows)
        d_x = d_out.astype(jnp.float32)
        grads_by_layer = [None] * layers
        tables_by_layer = [None] * layers
        for layer_idx in reversed(range(layers)):
            d_x, grads, d_rows = layer_bwd(d_x, saved_list[layer_idx], rows_list[layer_idx], w_up[layer_idx], w_down[layer_idx], w_gate[layer_idx], w_proj[layer_idx])
            grad_send = jnp.zeros((shards * cap_rows, d_rows.shape[1]), jnp.float32).at[dest_slot].set(d_rows)
            grad_recv = lax.all_to_all(grad_send, "emb", 0, 0, tiled=True)
            tables_by_layer[layer_idx] = jax.ops.segment_sum(grad_recv, req_recv, num_segments=rows_dev)
            grads_by_layer[layer_idx] = lax.psum(grads, "emb")
        grad_stacks = [jnp.stack([entry[grad_pos] for entry in grads_by_layer]) for grad_pos in range(4)]
        return (x_cur, jnp.stack(tables_by_layer), grad_stacks[0], grad_stacks[1], grad_stacks[2], grad_stacks[3])

    return jax.shard_map(
        device_step,
        mesh=mesh,
        in_specs=(P("emb"), P("emb", None), P("emb", None), P(None, "emb", None), P(), P(), P(), P()),
        out_specs=(P("emb", None), P(None, "emb", None), P(), P(), P(), P()),
        check_vma=False,
    )
```

profile of v0, /device:TPU:0, one launch (start us, length us, event | category | flops | bytes accessed | tf_op | source)
XLA Modules:
  0.0 2378.1 jit_solution(8617865037633595703)
XLA Ops:
  17.7 18.0 slice_bitcast_fusion
  35.8 14.6 gather_fusion.2
  50.4 14.6 gather_fusion.4
  65.0 14.6 gather_fusion
  79.6 14.6 gather_fusion.6
  94.2 11.4 broadcast_select_fusion
  127.4 35.8 %all-to-all-done.1 = bf16[16,128,1024]{2,1,0:T(8,128)(2,1)} async-done(((bf16[16,128,1024]{2,1,0:T(8,128)(2,1)}), bf16[16,128,1024]{2,1,0:T(8,128)(2,1)}, u32[]{:S(2)}, u32[]{:S(2)}) %all-to-all-start.1) | async-done | bytes 4194336 | tf_op jit(solution)/shard_map/all_to_all | solution.py:71
  167.6 11.0 fusion.268
  203.0 18.1 all-to-all-done.2
  231.5 10.4 fusion.271
  259.6 19.9 all-to-all-done.3
  289.7 10.4 fusion.274
  317.3 20.1 all-to-all-done.4
  342.9 12.8 fusion.6
  371.2 11.8 fusion.9
  412.9 11.7 fusion.12
  535.1 17.9 convolution_bitcast_fusion.7
  573.0 123.2 %all-to-all-done.5 = f32[16,128,1024]{2,1,0:T(8,128)} async-done(((f32[16,128,1024]{2,1,0:T(8,128)}), f32[16,128,1024]{2,1,0:T(8,128)}, u32[]{:S(2)}, u32[]{:S(2)}) %all-to-all-start.5) | async-done | bytes 8388640 | tf_op jit(solution)/shard_map/all_to_all | solution.py:82
  710.6 119.8 %all-to-all-done.6 = f32[16,128,1024]{2,1,0:T(8,128)} async-done(((f32[16,128,1024]{2,1,0:T(8,128)}), f32[16,128,1024]{2,1,0:T(8,128)}, u32[]{:S(2)}, u32[]{:S(2)}) %all-to-all-start.6) | async-done | bytes 8388640 | tf_op jit(solution)/shard_map/all_to_all | solution.py:82
  841.5 116.1 %all-to-all-done.7 = f32[16,128,1024]{2,1,0:T(8,128)} async-done(((f32[16,128,1024]{2,1,0:T(8,128)}), f32[16,128,1024]{2,1,0:T(8,128)}, u32[]{:S(2)}, u32[]{:S(2)}) %all-to-all-start.7) | async-done | bytes 8388640 | tf_op jit(solution)/shard_map/all_to_all | solution.py:82
  977.8 24.7 %scatter_custom_fusion.2 = f32[3144,1024]{1,0:T(8,128)} fusion(s32[2048]{0:T(1024)} %bitcast.280, f32[2048,1024]{1,0:T(8,128)} %bitcast.34, f32[]{:T(128)} %constant.33.clone.1), kind=kCustom, calls=%fused_computation.149 | custom fusion | flops 2097152 | bytes 12878336 | tf_op jit(solution)/shard_map/scatter-add | solution.py:83
  1002.5 24.5 %scatter_custom_fusion.4 = f32[3144,1024]{1,0:T(8,128)} fusion(s32[2048]{0:T(1024)} %bitcast.281, f32[2048,1024]{1,0:T(8,128)} %bitcast.37, f32[]{:T(128)} %constant.33.clone.1), kind=kCustom, calls=%fused_computation.147 | custom fusion | flops 2097152 | bytes 12878336 | tf_op jit(solution)/shard_map/scatter-add | solution.py:83
  1026.9 24.5 %scatter_custom_fusion.6 = f32[3144,1024]{1,0:T(8,128)} fusion(s32[2048]{0:T(1024)} %bitcast.282, f32[2048,1024]{1,0:T(8,128)} %bitcast.40, f32[]{:T(128)} %constant.33.clone.1), kind=kCustom, calls=%fused_computation.145 | custom fusion | flops 2097152 | bytes 12878336 | tf_op jit(solution)/shard_map/scatter-add | solution.py:83
  1051.4 43.8 %all-to-all-done.8 = f32[16,128,1024]{2,1,0:T(8,128)} async-done(((f32[16,128,1024]{2,1,0:T(8,128)}), f32[16,128,1024]{2,1,0:T(8,128)}, u32[]{:S(2)}, u32[]{:S(2)}) %all-to-all-start.8) | async-done | bytes 8388640 | tf_op jit(solution)/shard_map/all_to_all | solution.py:82
  1095.3 24.4 %scatter_custom_fusion.8 = f32[3144,1024]{1,0:T(8,128)} fusion(s32[2048]{0:T(1024)} %bitcast.283, f32[2048,1024]{1,0:T(8,128)} %bitcast.43, f32[]{:T(128)} %constant.33.clone.1), kind=kCustom, calls=%fused_computation.143 | custom fusion | flops 2097152 | bytes 12878336 | tf_op jit(solution)/shard_map/scatter-add | solution.py:83
  1119.6 34.6 %pad_maximum_fusion.2 = f32[4,3144,1024]{2,1,0:T(8,128)} fusion(f32[1,3144,1024]{2,1,0:T(8,128)} %bitcast.269, f32[1,3144,1024]{2,1,0:T(8,128)} %bitcast.268, f32[1,3144,1024]{2,1,0:T(8,128)} %bitcast.267, f32[1,3144,1024]{2,1,0:T(8,128)} %bitcast.266), kind=kLoop, calls=%fused_computation.19 | loop fusion | flops 38633472 | bytes 103022592 | tf_op jit(solution)/shard_map/stack | solution.py:86
  1154.3 51.3 %all-reduce.7.cloned.1.call-done = (f32[1,4096,1024]{2,1,0:T(8,128)}, f32[1,1024,1024]{2,1,0:T(8,128)}, f32[1,1024,1024]{2,1,0:T(8,128)}, f32[1,1024,1024]{2,1,0...) async-done(((f32[1,4096,1024]{2,1,0:T(8,128)}, f32[1,1024,1024]{2,1,0:T(8,128)}, f32[1,1024,1024]{2,1,0:T(8,128)}, ...) | async-done | bytes 41943056 | tf_op jit(solution)/shard_map/psum | solution.py:84
  1205.6 12.0 pad_maximum_fusion.4
  1217.5 1052.9 %all-reduce.5.cloned.1.call-done = (f32[1,1024,4096]{2,1,0:T(8,128)}, f32[1,1024,4096]{2,1,0:T(8,128)}, f32[1,1024,4096]{2,1,0:T(8,128)}, f32[1,1024,4096]{2,1,0...) async-done(((f32[1,1024,4096]{2,1,0:T(8,128)}, ...) | async-done | bytes 125829136 | tf_op jit(solution)/shard_map/psum | solution.py:84
  2270.4 12.0 pad_maximum_fusion.3
  2282.3 44.4 %pad_maximum_fusion.1 = f32[4,4096,1024]{2,1,0:T(8,128)} fusion(f32[1,4096,1024]{2,1,0:T(8,128)} %get-tuple-element.12, f32[1,4096,1024]{2,1,0:T(8,128)} %get-tuple-element.13, f32[1,4096,1024]{2,1,0:T(8,128)} %get-tuple-element.14, f32[1,4096,1024]{2,1,0:T(8,128)} %get-tuple-element.17), kind=kLoop, calls=%fused_computation.18 | loop fusion | flops 50331648 | bytes 134217728 | tf_op jit(solution)/shard_map/stack | solution.py:85
  2326.8 44.0 %pad_maximum_fusion = f32[4,1024,4096]{2,1,0:T(8,128)} fusion(f32[1,1024,4096]{2,1,0:T(8,128)} %get-tuple-element.8, f32[1,1024,4096]{2,1,0:T(8,128)} %get-tuple-element.9, f32[1,1024,4096]{2,1,0:T(8,128)} %get-tuple-element.10, f32[1,1024,4096]{2,1,0:T(8,128)} %get-tuple-element.11), kind=kLoop, calls=%fused_computation.17 | loop fusion | flops 50331648 | bytes 134217728 | tf_op jit(solution)/shard_map/stack | solution.py:85
  (219 shorter events, 342.9 us)
Async XLA Ops:
  9.4 100.3 %copy-start.50 = (s32[512]{0:T(512)}, s32[512]{0:T(512)S(1)}, u32[]{:S(2)}) copy-start(s32[512]{0:T(512)S(1)} %get-tuple-element.27) | copy-start | bytes 6148
  9.4 465.4 %copy-start.54 = (pred[512]{0:T(512)(128)(4,1)}, pred[512]{0:T(512)(128)(4,1)S(1)}, u32[]{:S(2)}) copy-start(pred[512]{0:T(512)(128)(4,1)S(1)} %get-tuple-element.26) | copy-start | bytes 1540
  12.4 23.3 all-to-all-start
  35.8 14.6 copy-start.46
  105.6 57.6 %all-to-all-start.1 = ((bf16[16,128,1024]{2,1,0:T(8,128)(2,1)}), bf16[16,128,1024]{2,1,0:T(8,128)(2,1)}, u32[]{:S(2)}, u32[]{:S(2)}) async-start(bf16[16,128,1024]{2,1,0:T(8,128)(2,1)} %bitcast.277), calls=%async_computation.1 | async-start | bytes 8388608 | tf_op jit(solution)/shard_map/all_to_all | solution.py:71
  163.2 57.9 %all-to-all-start.2 = ((bf16[16,128,1024]{2,1,0:T(8,128)(2,1)}), bf16[16,128,1024]{2,1,0:T(8,128)(2,1)}, u32[]{:S(2)}, u32[]{:S(2)}) async-start(bf16[16,128,1024]{2,1,0:T(8,128)(2,1)} %bitcast.276), calls=%async_computation.2 | async-start | bytes 8388608 | tf_op jit(solution)/shard_map/all_to_all | solution.py:71
  188.9 53.0 %copy-start.4 = (bf16[512,1024]{1,0:T(8,128)(2,1)}, bf16[512,1024]{1,0:T(8,128)(2,1)S(1)}, u32[]{:S(2)}) copy-start(bf16[512,1024]{1,0:T(8,128)(2,1)S(1)} %get-tuple-element.45) | copy-start | bytes 3145732
  221.1 58.4 %all-to-all-start.3 = ((bf16[16,128,1024]{2,1,0:T(8,128)(2,1)}), bf16[16,128,1024]{2,1,0:T(8,128)(2,1)}, u32[]{:S(2)}, u32[]{:S(2)}) async-start(bf16[16,128,1024]{2,1,0:T(8,128)(2,1)} %bitcast.275), calls=%async_computation.3 | async-start | bytes 8388608 | tf_op jit(solution)/shard_map/all_to_all | solution.py:71
  231.5 10.4 copy-start.11
  231.5 10.4 copy-start.24
  279.5 57.9 %all-to-all-start.4 = ((bf16[16,128,1024]{2,1,0:T(8,128)(2,1)}), bf16[16,128,1024]{2,1,0:T(8,128)(2,1)}, u32[]{:S(2)}, u32[]{:S(2)}) async-start(bf16[16,128,1024]{2,1,0:T(8,128)(2,1)} %bitcast.274), calls=%async_computation.4 | async-start | bytes 8388608 | tf_op jit(solution)/shard_map/all_to_all | solution.py:71
  283.9 921.6 %all-reduce.7.cloned.1.call-start = ((), (), s32[]{:S(2)}) async-start(), calls=%async_computation.10 | async-start | bytes 83886080 | tf_op jit(solution)/shard_map/psum | solution.py:84
  289.6 10.4 copy-start.9
  289.6 10.4 copy-start.31
  289.6 10.4 copy-start.37
  342.9 12.8 copy-start.1
  342.9 12.8 copy-start.19
  342.9 12.8 copy-start.27
  371.2 37.8 %copy-start.17 = (bf16[512,1024]{1,0:T(8,128)(2,1)}, bf16[512,1024]{1,0:T(8,128)(2,1)S(1)}, u32[]{:S(2)}) copy-start(bf16[512,1024]{1,0:T(8,128)(2,1)S(1)} %fusion.391) | copy-start | bytes 3145732
  401.7 11.1 copy-start.44
  405.1 24.3 %copy-start.40 = (bf16[512,1024]{1,0:T(8,128)(2,1)}, bf16[512,1024]{1,0:T(8,128)(2,1)S(1)}, u32[]{:S(2)}) copy-start(bf16[512,1024]{1,0:T(8,128)(2,1)S(1)} %fusion.295) | copy-start | bytes 3145732
  412.9 11.7 copy-start.5
  412.9 11.7 copy-start.48
  445.1 18.0 copy-start.42
  449.0 10.3 copy-start.2
  449.0 10.3 copy-start.28
  467.8 1802.6 %all-reduce.5.cloned.1.call-start = ((), (), s32[]{:S(2)}) async-start(), calls=%async_computation.9 | async-start | bytes 251658240 | tf_op jit(solution)/shard_map/psum | solution.py:84
  561.5 134.7 %all-to-all-start.5 = ((f32[16,128,1024]{2,1,0:T(8,128)}), f32[16,128,1024]{2,1,0:T(8,128)}, u32[]{:S(2)}, u32[]{:S(2)}) async-start(f32[16,128,1024]{2,1,0:T(8,128)} %bitcast.273), calls=%async_computation.5 | async-start | bytes 16777216 | tf_op jit(solution)/shard_map/all_to_all | solution.py:82
  696.2 134.2 %all-to-all-start.6 = ((f32[16,128,1024]{2,1,0:T(8,128)}), f32[16,128,1024]{2,1,0:T(8,128)}, u32[]{:S(2)}, u32[]{:S(2)}) async-start(f32[16,128,1024]{2,1,0:T(8,128)} %bitcast.271), calls=%async_computation.6 | async-start | bytes 16777216 | tf_op jit(solution)/shard_map/all_to_all | solution.py:82
  830.4 127.2 %all-to-all-start.7 = ((f32[16,128,1024]{2,1,0:T(8,128)}), f32[16,128,1024]{2,1,0:T(8,128)}, u32[]{:S(2)}, u32[]{:S(2)}) async-start(f32[16,128,1024]{2,1,0:T(8,128)} %bitcast.272), calls=%async_computation.7 | async-start | bytes 16777216 | tf_op jit(solution)/shard_map/all_to_all | solution.py:82
  957.6 137.7 %all-to-all-start.8 = ((f32[16,128,1024]{2,1,0:T(8,128)}), f32[16,128,1024]{2,1,0:T(8,128)}, u32[]{:S(2)}, u32[]{:S(2)}) async-start(f32[16,128,1024]{2,1,0:T(8,128)} %bitcast.270), calls=%async_computation.8 | async-start | bytes 16777216 | tf_op jit(solution)/shard_map/all_to_all | solution.py:82
  963.3 10.1 copy-start.3
  (47 other events, 274.1 us)
Sparse Core Ops, SparseCore 0:
  467.9 737.5 all-reduce.6
  1212.6 1057.7 all-reduce.4
where the time goes:
time: 2390 us; the launch traced here: 2380 us
  waiting for transfers between devices  1600 us (67%)
  matrix products  320 us (13%)
  other arithmetic  291 us (12%)
  local copies, waits for them, and re-layouts  106 us (4%)
  starting transfers between devices  44.8 us (2%)
    psum x2, waiting for transfers between devices, device_step(): grads_by_layer[layer_idx] = lax.psum(grads, 'emb')  1100 us
    all_to_all x4, waiting for transfers between devices, device_step(): grad_recv = lax.all_to_all(grad_send, 'emb', 0, 0, tiled=True)  403 us
    another operation x4, other arithmetic, device_step(): jnp.stack([entry[grad_pos] for entry in grads_by_layer])  112 us
    scatter-add x4, other arithmetic, device_step(): jax.ops.segment_sum(grad_recv, req_recv, num_segments=rows_dev)  98 us
    all_to_all x4, waiting for transfers between devices, device_step(): returned = lax.all_to_all(served, 'emb', 0, 0, tiled=True)  93.9 us
    gather x4, local copies, waits for them, and re-layouts, device_step(): served = jnp.take(ple_tables[layer_idx], req_recv, axis=0)  58.4 us
  transfers between devices with their start and end apart: 11, of which 10 were waited for; matrix products, arithmetic and copies ran while one was open for 17% of the time, Pallas kernels for 0%

commit v1 on v0

v1 whole, which is shorter than its diff:
```python
import jax
import jax.numpy as jnp
from jax import lax
from jax.experimental import pallas as pl
from jax.experimental.pallas import tpu as pltpu
from jax.sharding import PartitionSpec as P


EPS = 1e-6
CAP_DIV = 4
CORE, X, Y, Z = 1, 2, 4, 8
GROUP = 4


def gelu_tanh(pre_act):
    return jax.nn.gelu(pre_act, approximate=True)


def gelu_back(pre_act, grad_out):
    _, pull_back = jax.vjp(gelu_tanh, pre_act.astype(jnp.float32))
    return pull_back(grad_out.astype(jnp.float32))[0]


def dot32(spec, a, b):
    return jnp.einsum(spec, a, b, preferred_element_type=jnp.float32)


def layer_fwd(x_cur, up_mat, down_mat, gate_mat, proj_mat, emb_rows):
    x_wide = x_cur.astype(jnp.float32)
    inv_rms = lax.rsqrt(jnp.mean(x_wide * x_wide, axis=-1, keepdims=True) + EPS)
    normed = (x_wide * inv_rms).astype(jnp.bfloat16)
    hidden = dot32("nd,df->nf", normed, up_mat).astype(jnp.bfloat16)
    act_out = gelu_tanh(hidden.astype(jnp.float32)).astype(jnp.bfloat16)
    mlp_out = dot32("nf,fd->nd", act_out, down_mat).astype(jnp.bfloat16)
    gate_pre = dot32("nd,de->ne", normed, gate_mat).astype(jnp.bfloat16)
    gate_act = gelu_tanh(gate_pre.astype(jnp.float32)).astype(jnp.bfloat16)
    mix_rows = (gate_act.astype(jnp.float32) * emb_rows.astype(jnp.float32)).astype(jnp.bfloat16)
    ple_out = dot32("ne,ed->nd", mix_rows, proj_mat).astype(jnp.bfloat16)
    x_next = (x_wide + mlp_out.astype(jnp.float32) + ple_out.astype(jnp.float32)).astype(jnp.bfloat16)
    return x_next, (x_wide, inv_rms, normed, hidden, gate_pre, gate_act)


def layer_bwd(d_x, g_out, saved, emb_rows, up_mat, down_mat, gate_mat, proj_mat, need_dx):
    x_wide, inv_rms, _, hidden, gate_pre, gate_act = saved
    d_mix = dot32("nd,ed->ne", g_out, proj_mat).astype(jnp.bfloat16)
    d_rows = gate_act.astype(jnp.float32) * d_mix.astype(jnp.float32)
    if not need_dx:
        return None, d_rows
    d_act = dot32("nd,fd->nf", g_out, down_mat).astype(jnp.bfloat16)
    d_hidden = gelu_back(hidden, d_act).astype(jnp.bfloat16)
    d_gate_act = (emb_rows.astype(jnp.float32) * d_mix.astype(jnp.float32)).astype(jnp.bfloat16)
    d_gate_pre = gelu_back(gate_pre, d_gate_act).astype(jnp.bfloat16)
    d_norm = dot32("nf,df->nd", d_hidden, up_mat) + dot32("ne,de->nd", d_gate_pre, gate_mat)
    d_x_new = d_x + inv_rms * d_norm - inv_rms ** 3 * x_wide * jnp.mean(d_norm * x_wide, axis=-1, keepdims=True)
    return d_x_new, d_rows


def cost(nbytes):
    return pl.CostEstimate(flops=int(nbytes), bytes_accessed=int(nbytes), transcendentals=0)


def weight_slices(quarter, w_up, w_gate, w_down, w_proj, blocks):
    layers, dim, hid = w_up.shape
    emb = w_gate.shape[2]
    hb, eb = hid // (GROUP * blocks), emb // (GROUP * blocks)

    def body(q_ref, up_ref, down_ref, proj_ref, up_out, down_out, proj_out):
        up_out[...] = up_ref[...]
        down_out[...] = down_ref[...]
        proj_out[...] = proj_ref[...]

    return pl.pallas_call(
        body,
        grid_spec=pltpu.PrefetchScalarGridSpec(
            num_scalar_prefetch=1,
            grid=(layers, blocks),
            in_specs=[
                pl.BlockSpec((1, dim, hb), lambda l, j, q: (l, 0, GROUP * j + q[0])),
                pl.BlockSpec((1, hb, dim), lambda l, j, q: (l, GROUP * j + q[0], 0)),
                pl.BlockSpec((1, eb, dim), lambda l, j, q: (l, GROUP * j + q[0], 0)),
            ],
            out_specs=[
                pl.BlockSpec((1, dim, hb), lambda l, j, q: (l, 0, j)),
                pl.BlockSpec((1, hb, dim), lambda l, j, q: (l, j, 0)),
                pl.BlockSpec((1, eb, dim), lambda l, j, q: (l, j, 0)),
            ],
        ),
        out_shape=[
            jax.ShapeDtypeStruct((layers, dim, hid // GROUP), w_up.dtype),
            jax.ShapeDtypeStruct((layers, hid // GROUP, dim), w_up.dtype),
            jax.ShapeDtypeStruct((layers, emb // GROUP, dim), w_up.dtype),
        ],
        cost_estimate=cost(4 * layers * dim * (2 * hid + emb) // GROUP),
        name="weight_slices",
    )(quarter, w_up, w_down, w_proj)


def blank(shapes):
    return pl.pallas_call(
        lambda *refs: None,
        out_shape=[jax.ShapeDtypeStruct(shape, jnp.float32) for shape in shapes],
        out_specs=[pl.BlockSpec(memory_space=pl.ANY)] * len(shapes),
        name="blank",
    )()


def place_cols(layer, buf, out_main, out_side):
    n, rows, dim = buf.shape
    hb = out_main.shape[2] // n
    eb = rows - hb
    at_once = max(1, 128 // eb)

    def body(buf_ref, main_in, side_in, main_ref, side_ref):
        for j in range(at_once):
            main_ref[0, :, j * hb:(j + 1) * hb] = buf_ref[j, :hb].T
        side = jnp.concatenate([buf_ref[j, hb:] for j in range(at_once)], axis=0)
        side_ref[0] = side.T

    return pl.pallas_call(
        body,
        grid=(n // at_once,),
        in_specs=[
            pl.BlockSpec((at_once, rows, dim), lambda j: (j, 0, 0)),
            pl.BlockSpec(memory_space=pl.ANY),
            pl.BlockSpec(memory_space=pl.ANY),
        ],
        out_specs=[
            pl.BlockSpec((1, dim, at_once * hb), lambda j: (layer, 0, j)),
            pl.BlockSpec((1, dim, at_once * eb), lambda j: (layer, 0, j)),
        ],
        out_shape=[
            jax.ShapeDtypeStruct(out_main.shape, out_main.dtype),
            jax.ShapeDtypeStruct(out_side.shape, out_side.dtype),
        ],
        input_output_aliases={1: 0, 2: 1},
        cost_estimate=cost(8 * n * rows * dim),
        name="place_cols",
    )(buf, out_main, out_side)


def place_rows(layer, buf, out_main, out_side):
    n, rows, dim = buf.shape
    hb = out_main.shape[1] // n
    eb = rows - hb
    at_once = 2

    def body(buf_ref, main_in, side_in, main_ref, side_ref):
        for j in range(at_once):
            main_ref[0, j * hb:(j + 1) * hb] = buf_ref[j, :hb]
            side_ref[0, j * eb:(j + 1) * eb] = buf_ref[j, hb:]

    return pl.pallas_call(
        body,
        grid=(n // at_once,),
        in_specs=[
            pl.BlockSpec((at_once, rows, dim), lambda j: (j, 0, 0)),
            pl.BlockSpec(memory_space=pl.ANY),
            pl.BlockSpec(memory_space=pl.ANY),
        ],
        out_specs=[
            pl.BlockSpec((1, at_once * hb, dim), lambda j: (layer, j, 0)),
            pl.BlockSpec((1, at_once * eb, dim), lambda j: (layer, j, 0)),
        ],
        out_shape=[
            jax.ShapeDtypeStruct(out_main.shape, out_main.dtype),
            jax.ShapeDtypeStruct(out_side.shape, out_side.dtype),
        ],
        input_output_aliases={1: 0, 2: 1},
        cost_estimate=cost(8 * n * rows * dim),
        name="place_rows",
    )(buf, out_main, out_side)


def place_table(layer, table, out):
    rows, dim = table.shape
    steps = 3 if rows % 24 == 0 else 1

    def body(table_ref, out_in, out_ref):
        out_ref[0] = table_ref[...]

    return pl.pallas_call(
        body,
        grid=(steps,),
        in_specs=[
            pl.BlockSpec((rows // steps, dim), lambda j: (j, 0)),
            pl.BlockSpec(memory_space=pl.ANY),
        ],
        out_specs=pl.BlockSpec((1, rows // steps, dim), lambda j: (layer, j, 0)),
        out_shape=jax.ShapeDtypeStruct(out.shape, out.dtype),
        input_output_aliases={1: 0},
        cost_estimate=cost(8 * rows * dim),
        name="place_table",
    )(table, out)


def solution(mesh):
    shards = mesh.shape["emb"]

    def swap(arr, axis_bit):
        return lax.ppermute(arr, "emb", [(dev, dev ^ axis_bit) for dev in range(shards)])

    def device_step(tok_ids, x_in, d_out, ple_tables, w_up, w_down, w_gate, w_proj):
        layers, rows_dev, emb_dim = ple_tables.shape
        me = lax.axis_index("emb")
        quarter = me % GROUP
        y_pos, z_pos = (me // Y) % 2, (me // Z) % 2
        cap_rows = tok_ids.shape[0] // CAP_DIV
        owner_dev = tok_ids // rows_dev
        local_row = tok_ids - owner_dev * rows_dev
        owner_hot = (owner_dev[:, None] == jnp.arange(shards, dtype=jnp.int32)[None, :]).astype(jnp.int32)
        slot_rank = jnp.sum((jnp.cumsum(owner_hot, axis=0) - owner_hot) * owner_hot, axis=1)
        dest_slot = owner_dev * cap_rows + slot_rank
        req_send = jnp.zeros((shards * cap_rows,), jnp.int32).at[dest_slot].set(local_row)
        req_recv = lax.all_to_all(req_send, "emb", 0, 0, tiled=True)
        sync = lax.optimization_barrier
        blocks = shards // GROUP

        def group(arr):
            twin = swap(arr, X)
            pair = jnp.concatenate([arr, twin], axis=-2)
            twin = swap(pair, CORE)
            return jnp.concatenate([pair, twin], axis=-2)

        last = layers - 1
        x_cur = x_in
        saved_list, rows_list, acts_list = [], [], []
        o_last = group(d_out)
        for layer in range(layers):
            served = jnp.take(ple_tables[layer], req_recv, axis=0)
            returned = lax.all_to_all(served, "emb", 0, 0, tiled=True)
            emb_rows = jnp.take(returned, dest_slot, axis=0)
            x_cur, saved = layer_fwd(x_cur, w_up[layer], w_down[layer], w_gate[layer], w_proj[layer], emb_rows)
            saved_list.append(saved)
            rows_list.append(emb_rows)
            acts_list.append(jnp.stack([saved[2], emb_rows]))
            if layer == 0:
                x_cur, o_last = sync((x_cur, o_last))
        x_out, acts_list = sync((x_cur, acts_list))

        def side_cols(arr):
            wide = arr.shape[-1]
            cut = arr.reshape(arr.shape[:-1] + (blocks, GROUP, wide // (blocks * GROUP)))
            pick = (jnp.arange(GROUP) == quarter)[:, None]
            return jnp.sum(jnp.where(pick, cut, 0), axis=-2).reshape(arr.shape[:-1] + (wide // GROUP,))

        def dx_step(layer, d_x):
            g_out = d_x.astype(jnp.bfloat16)
            d_x, d_rows = layer_bwd(d_x, g_out, saved_list[layer], rows_list[layer], w_up[layer], w_down[layer], w_gate[layer], w_proj[layer], layer > 0)
            return d_x, jnp.zeros((shards * cap_rows, emb_dim), jnp.float32).at[dest_slot].set(d_rows)

        def grads_head(layer, ue, o_rows):
            u_rows, e_part = ue[0], side_cols(ue[1])
            h_pre = dot32("nd,df->nf", u_rows, up_q[layer]).astype(jnp.bfloat16)
            z_pre = dot32("nd,de->ne", u_rows, gate_q[layer]).astype(jnp.bfloat16)
            d_act = dot32("nd,fd->nf", o_rows, down_q[layer]).astype(jnp.bfloat16)
            d_mix = dot32("nd,ed->ne", o_rows, proj_q[layer]).astype(jnp.bfloat16)
            act = gelu_tanh(h_pre.astype(jnp.float32)).astype(jnp.bfloat16)
            gate = gelu_tanh(z_pre.astype(jnp.float32)).astype(jnp.bfloat16)
            mix = (gate.astype(jnp.float32) * e_part.astype(jnp.float32)).astype(jnp.bfloat16)
            d_hid = gelu_back(h_pre, d_act).astype(jnp.bfloat16)
            d_gate = (e_part.astype(jnp.float32) * d_mix.astype(jnp.float32)).astype(jnp.bfloat16)
            d_pre = gelu_back(z_pre, d_gate).astype(jnp.bfloat16)
            return u_rows, o_rows, d_hid, d_pre, act, mix

        def grads_tail(u_rows, o_rows, d_hid, d_pre, act, mix):
            grads = [dot32("nf,nd->fd", lhs, rhs) for lhs, rhs in ((d_hid, u_rows), (d_pre, u_rows), (act, o_rows), (mix, o_rows))]
            return [g.reshape(2, 2, -1, g.shape[1]) for g in grads]

        def take(arrs, positions, axes):
            return [lax.dynamic_index_in_dim(arr, pos, axis=ax, keepdims=False) for arr, pos, ax in zip(arrs, positions, axes)]

        def sum_with(mine, sent, bits):
            return [own + swap(arr, bit) for own, arr, bit in zip(mine, sent, bits)]

        outs = blank([w_up.shape, w_gate.shape, w_down.shape, w_proj.shape, ple_tables.shape])
        col_outs, row_outs, table_out = (outs[0], outs[1]), (outs[2], outs[3]), outs[4]
        up_q, down_q, proj_q = weight_slices(quarter[None], w_up, w_gate, w_down, w_proj, blocks)
        gate_q = side_cols(w_gate)
        d_x = d_out.astype(jnp.float32)
        ue_last = group(acts_list[last])
        d_x, slots = dx_step(last, d_x)
        d_x, slots, ue_last, o_last = sync((d_x, slots, ue_last, o_last))
        recv = lax.all_to_all(slots, "emb", 0, 0, tiled=True)
        grads = grads_tail(*grads_head(last, ue_last, o_last))
        gathered = {}
        way1, way2 = (Y, Y, Z, Z), (Z, Z, Y, Y)
        pos1, pos2 = (y_pos, y_pos, z_pos, z_pos), (z_pos, z_pos, y_pos, y_pos)
        not1, not2 = [1 - p for p in pos1], [1 - p for p in pos2]
        for layer in reversed(range(layers)):
            sent = take(grads, not1, (1, 1, 0, 0))
            sent, grads, d_x = sync((sent, grads, d_x))
            sums = sum_with(take(grads, pos1, (1, 1, 0, 0)), sent, way1)
            if layer > 0:
                o_next = group(d_x.astype(jnp.bfloat16))
                ue_next = group(acts_list[layer - 1])
                d_x, slots = dx_step(layer - 1, d_x)
                sums, d_x, slots, o_next, ue_next, recv = sync((sums, d_x, slots, o_next, ue_next, recv))
            else:
                sums, recv = sync((sums, recv))
            sent = take(sums, not2, (0, 0, 0, 0))
            sent, sums = sync((sent, sums))
            sums = sum_with(take(sums, pos2, (0, 0, 0, 0)), sent, way2)
            table = jax.ops.segment_sum(recv, req_recv, num_segments=rows_dev)
            table_out = place_table(layer, table, table_out)
            if layer > 0:
                recv = lax.all_to_all(slots, "emb", 0, 0, tiled=True)
                head = grads_head(layer - 1, ue_next, o_next)
                sums, head, table_out = sync((sums, head, table_out))
            else:
                sums = sync(sums)
            cols_piece = jnp.concatenate(sums[:2], axis=0)
            rows_piece = jnp.concatenate(sums[2:], axis=0)
            if layer + 2 in gathered:
                ready = gathered.pop(layer + 2)
                col_outs = place_cols(layer + 2, ready[0], *col_outs)
                row_outs = place_rows(layer + 2, ready[1], *row_outs)
            if layer > 0:
                grads = grads_tail(*head)
            gathered[layer] = (lax.all_gather(cols_piece, "emb"), lax.all_gather(rows_piece, "emb"))
        for layer in sorted(gathered, reverse=True):
            cols_all, rows_all = gathered[layer]
            col_outs = place_cols(layer, cols_all, *col_outs)
            row_outs = place_rows(layer, rows_all, *row_outs)
        return (x_out, table_out, col_outs[0], row_outs[0], col_outs[1], row_outs[1])

    return jax.shard_map(
        device_step,
        mesh=mesh,
        in_specs=(P("emb"), P("emb", None), P("emb", None), P(None, "emb", None), P(), P(), P(), P()),
        out_specs=(P("emb", None), P(None, "emb", None), P(), P(), P(), P()),
        check_vma=False,
    )
```

time: 2390 us -> 2200 us (0.921)
  waiting for transfers between devices: 1600 us -> 1020 us
  Pallas kernels: 0 us -> 196 us
  local copies, waits for them, and re-layouts: 106 us -> 215 us
  matrix products: 320 us -> 373 us
  starting transfers between devices: 44.8 us -> 85.2 us
    psum x2 -> x0, waiting for transfers between devices: 1100 us -> none  [device_step(): grads_by_layer[layer_idx] = lax.psum(grads, 'emb')]
    ppermute x0 -> x48, waiting for transfers between devices: none -> 888 us  [swap(): lax.ppermute(arr, 'emb', [(dev, dev ^ axis_bit) for dev in range(shards)])]
    all_to_all x4, waiting for transfers between devices: 403 us -> 0.01 us  [device_step(): recv = lax.all_to_all(slots, 'emb', 0, 0, tiled=True)]
    pallas_call x0 -> x14, Pallas kernels: none -> 196 us  [the longest x4 70.5 us: place_cols(): pl.pallas_call(body, grid=(n // at_once,), in_specs=[pl.BlockSpec((at_onc...]
    another operation x7 -> x8, other arithmetic: 148 us -> 13.4 us  [the longest x6 12.2 us: device_step(): acts_list.append(jnp.stack([saved[2], emb_rows]))]
    all_gather x0 -> x8, waiting for transfers between devices: none -> 84.5 us  [the longest x4 76.1 us: device_step(): lax.all_gather(cols_piece, 'emb')]
    concatenate x0 -> x24, other arithmetic: none -> 61.2 us  [the longest x8 34.7 us: group(): return jnp.concatenate([pair, twin], axis=-2)]
    dot_general x45 -> x57, matrix products: 320 us -> 373 us  [dot32(): return jnp.einsum(spec, a, b, preferred_element_type=jnp.float32)]
  transfers between devices with their start and end apart: 11 -> 65, of which waited for: 10 -> 23; matrix products, arithmetic and copies ran while one was open for 17% -> 31% of each run, Pallas kernels for 0% -> 8%
where the time goes in v1:
time: 2200 us; the launch traced here: 2190 us
  waiting for transfers between devices  1020 us (46%)
  matrix products  373 us (17%)
  other arithmetic  279 us (13%)
  local copies, waits for them, and re-layouts  215 us (10%)
  Pallas kernels  196 us (9%)
  starting transfers between devices  85.2 us (4%)
    ppermute x48, waiting for transfers between devices, swap(): lax.ppermute(arr, 'emb', [(dev, dev ^ axis_bit) for dev in range(shards)])  888 us
    dot_general x57, matrix products, dot32(): return jnp.einsum(spec, a, b, preferred_element_type=jnp.float32)  373 us
    scatter-add x4, other arithmetic, device_step(): table = jax.ops.segment_sum(recv, req_recv, num_segments=rows_dev)  97.6 us
    all_gather x4, waiting for transfers between devices, device_step(): lax.all_gather(cols_piece, 'emb')  76.1 us
    pallas_call x4, Pallas kernels, place_cols(): pl.pallas_call(body, grid=(n // at_once,), in_specs=[pl.BlockSpec((at_onc...  70.5 us
    pallas_call x4, Pallas kernels, place_rows(): pl.pallas_call(body, grid=(n // at_once,), in_specs=[pl.BlockSpec((at_onc...  65.9 us
    gather x4, local copies, waits for them, and re-layouts, device_step(): served = jnp.take(ple_tables[layer], req_recv, axis=0)  58.4 us
    all_to_all x4, waiting for transfers between devices, device_step(): returned = lax.all_to_all(served, 'emb', 0, 0, tiled=True)  49.9 us
  transfers between devices with their start and end apart: 65, of which 23 were waited for; matrix products, arithmetic and copies ran while one was open for 31% of the time, Pallas kernels for 8%

profile of v1, /device:TPU:0, one launch (start us, length us, event | category | flops | bytes accessed | tf_op | source)
XLA Modules:
  0.0 2187.4 jit_solution(16349944078735601508)
XLA Ops:
  17.7 18.0 slice_bitcast_fusion
  112.1 74.2 %collective-permute-done = bf16[512,1024]{1,0:T(8,128)(2,1)S(1)} collective-permute-done((bf16[512,1024]{1,0:T(8,128)(2,1)S(1)}, bf16[512,1024]{1,0:T(8,128)(2,1)S(1)}, u32[]{:S(2)}, u32[]{:S(2)}) %collective-permute-start) | collective-permute-done | bytes 1048608 | tf_op jit(solution)/shard_map/ppermute | solution.py:200
  187.8 15.8 fusion.451
  244.3 16.5 all-to-all-done.2
  295.4 22.3 %all-to-all-done.3 = bf16[16,128,1024]{2,1,0:T(8,128)(2,1)} async-done(((bf16[16,128,1024]{2,1,0:T(8,128)(2,1)}), bf16[16,128,1024]{2,1,0:T(8,128)(2,1)}, u32[]{:S(2)}, u32[]{:S(2)}) %all-to-all-start.3) | async-done | bytes 4194336 | tf_op jit(solution)/shard_map/all_to_all | solution.py:230
  400.5 17.5 fusion.331
  433.7 45.7 %collective-permute-done.2 = bf16[2,512,1024]{2,1,0:T(8,128)(2,1)S(1)} collective-permute-done((bf16[2,512,1024]{2,1,0:T(8,128)(2,1)S(1)}, bf16[2,512,1024]{2,1,0:T(8,128)(2,1)S(1)}, u32[]{:S(2)}, u32[]{:S(2)}) %collective-permute-start.2) | collective-permute-done | bytes 2097184 | tf_op jit(solution)/shard_map/ppermute | solution.py:200
  495.2 18.4 weight_slices.1
  617.0 17.0 fusion.318
  644.2 75.2 %collective-permute-done.8 = bf16[512,1024]{1,0:T(8,128)(2,1)S(1)} collective-permute-done((bf16[512,1024]{1,0:T(8,128)(2,1)S(1)}, bf16[512,1024]{1,0:T(8,128)(2,1)S(1)}, u32[]{:S(2)}, u32[]{:S(2)}) %collective-permute-start.8) | collective-permute-done | bytes 1048608 | tf_op jit(solution)/shard_map/ppermute | solution.py:200
  748.5 18.4 collective-permute-done.4
  827.9 24.4 %scatter_custom_fusion.3.table_ref = f32[3144,1024]{1,0:T(8,128)} fusion(s32[2048]{0:T(1024)} %bitcast.639, f32[2048,1024]{1,0:T(8,128)} %bitcast.70, f32[]{:T(128)} %constant.276.clone.1), kind=kCustom, calls=%fused_computation.208 | custom fusion | flops 2097152 | bytes 12878336 | tf_op jit(solution)/shard_map/scatter-add | solution.py:303
  871.2 72.7 %collective-permute-done.22 = bf16[2,512,1024]{2,1,0:T(8,128)(2,1)S(1)} collective-permute-done((bf16[2,512,1024]{2,1,0:T(8,128)(2,1)}, bf16[2,512,1024]{2,1,0:T(8,128)(2,1)S(1)}, u32[]{:S(2)}, u32[]{:S(2)}) %collective-permute-start.22) | collective-permute-done | bytes 2097184 | tf_op jit(solution)/shard_map/ppermute | solution.py:200
  1006.5 115.5 %collective-permute-done.20 = bf16[512,1024]{1,0:T(8,128)(2,1)S(1)} collective-permute-done((bf16[512,1024]{1,0:T(8,128)(2,1)S(1)}, bf16[512,1024]{1,0:T(8,128)(2,1)S(1)}, u32[]{:S(2)}, u32[]{:S(2)}) %collective-permute-start.20) | collective-permute-done | bytes 1048608 | tf_op jit(solution)/shard_map/ppermute | solution.py:200
  1123.9 18.6 fusion.305
  1156.3 20.8 collective-permute-done.19
  1243.0 24.3 %scatter_custom_fusion.5.table_ref = f32[3144,1024]{1,0:T(8,128)} fusion(s32[2048]{0:T(1024)} %bitcast.640, f32[2048,1024]{1,0:T(8,128)} %bitcast.100, f32[]{:T(128)} %constant.276.clone.1), kind=kCustom, calls=%fused_computation.206 | custom fusion | flops 2097152 | bytes 12878336 | tf_op jit(solution)/shard_map/scatter-add | solution.py:303
  1290.7 67.3 %collective-permute-done.34 = bf16[2,512,1024]{2,1,0:T(8,128)(2,1)} collective-permute-done((bf16[2,512,1024]{2,1,0:T(8,128)(2,1)S(1)}, bf16[2,512,1024]{2,1,0:T(8,128)(2,1)}, u32[]{:S(2)}, u32[]{:S(2)}) %collective-permute-start.34) | collective-permute-done | bytes 2097184 | tf_op jit(solution)/shard_map/ppermute | solution.py:200
  1383.5 125.7 %collective-permute-done.32 = bf16[512,1024]{1,0:T(8,128)(2,1)S(1)} collective-permute-done((bf16[512,1024]{1,0:T(8,128)(2,1)S(1)}, bf16[512,1024]{1,0:T(8,128)(2,1)S(1)}, u32[]{:S(2)}, u32[]{:S(2)}) %collective-permute-start.32) | collective-permute-done | bytes 1048608 | tf_op jit(solution)/shard_map/ppermute | solution.py:200
  1605.3 24.5 %scatter_custom_fusion.7.table_ref = f32[3144,1024]{1,0:T(8,128)} fusion(s32[2048]{0:T(1024)} %bitcast.641, f32[2048,1024]{1,0:T(8,128)} %bitcast.130, f32[]{:T(128)} %constant.276.clone.1), kind=kCustom, calls=%fused_computation.204 | custom fusion | flops 2097152 | bytes 12878336 | tf_op jit(solution)/shard_map/scatter-add | solution.py:303
  1675.6 189.3 %collective-permute-done.43 = f32[2,64,1024]{2,1,0:T(8,128)S(1)} collective-permute-done((f32[2,64,1024]{2,1,0:T(8,128)S(1)}, f32[2,64,1024]{2,1,0:T(8,128)S(1)}, u32[]{:S(2)}, u32[]{:S(2)}) %collective-permute-start.43) | collective-permute-done | bytes 524320 | tf_op jit(solution)/shard_map/ppermute | solution.py:200
  1877.4 44.2 %collective-permute-done.47 = f32[64,1024]{1,0:T(8,128)S(1)} collective-permute-done((f32[64,1024]{1,0:T(8,128)S(1)}, f32[64,1024]{1,0:T(8,128)S(1)}, u32[]{:S(2)}, u32[]{:S(2)}) %collective-permute-start.47) | collective-permute-done | bytes 262176 | tf_op jit(solution)/shard_map/ppermute | solution.py:200
  1924.8 24.4 %scatter_custom_fusion.8.table_ref = f32[3144,1024]{1,0:T(8,128)} fusion(s32[2048]{0:T(1024)} %bitcast.642, f32[2048,1024]{1,0:T(8,128)} %bitcast.160, f32[]{:T(128)} %constant.276.clone.1), kind=kCustom, calls=%fused_computation.202 | custom fusion | flops 2097152 | bytes 12878336 | tf_op jit(solution)/shard_map/scatter-add | solution.py:303
  1959.4 16.1 place_rows.4
  1975.5 18.1 place_cols.4
  1993.6 16.1 place_rows.5
  2009.7 17.4 place_cols.5
  2027.1 17.4 place_rows.6
  2044.5 17.6 place_cols.6
  2070.6 16.3 place_rows.7
  2086.8 76.1 %all-gather.17.cloned.1.call-done = f32[5120,1024]{1,0:T(8,128)} async-done(((f32[320,1024]{1,0:T(8,128)}), f32[5120,1024]{1,0:T(8,128)}) %all-gather.17.cloned.1.call-update) | async-done | bytes 20971536 | tf_op jit(solution)/shard_map/all_gather | solution.py:319
  2162.9 17.4 place_cols.7
  (606 shorter events, 868.0 us)
Async XLA Ops:
  105.6 99.2 %all-to-all-start.1 = ((bf16[16,128,1024]{2,1,0:T(8,128)(2,1)}), bf16[16,128,1024]{2,1,0:T(8,128)(2,1)}, u32[]{:S(2)}, u32[]{:S(2)}) async-start(bf16[16,128,1024]{2,1,0:T(8,128)(2,1)} %bitcast.595), calls=%async_computation.1 | async-start | bytes 8388608 | tf_op jit(solution)/shard_map/all_to_all | solution.py:230
  109.8 76.5 %collective-permute-start = (bf16[512,1024]{1,0:T(8,128)(2,1)S(1)}, bf16[512,1024]{1,0:T(8,128)(2,1)S(1)}, u32[]{:S(2)}, u32[]{:S(2)}) collective-permute-start(bf16[512,1024]{1,0:T(8,128)(2,1)S(1)} %copy-done.14), channel_id=1, source_target_pairs={{0,2},{1,3},{2,0},{3,1},{4,6},{5,7},{6,4},{7,5},{8,10},{9,11},{10,... | collective-permute-start | bytes 3145736 | tf_op jit(solution)/shard_map/ppermute | solution.py:200
  535.1 184.6 %collective-permute-start.11 = (bf16[2,1024,1024]{2,1,0:T(8,128)(2,1)}, bf16[2,1024,1024]{2,1,0:T(8,128)(2,1)}, u32[]{:S(2)}, u32[]{:S(2)}) collective-permute-start(bf16[2,1024,1024]{2,1,0:T(8,128)(2,1)} %pad_maximum_fusion.7), channel_id=1, source_target_pairs={{0,1},{1,0},{2,3},{3,2},{4,5},{5,4},{6,7},{7,6},{8,9},{9,8},{10,11... | collective-permute-start | bytes 12582920 | tf_op jit(solution)/shard_map/ppermute | solution.py:200
  590.3 180.7 %all-to-all-start.5 = ((f32[16,128,1024]{2,1,0:T(8,128)}), f32[16,128,1024]{2,1,0:T(8,128)}, u32[]{:S(2)}, u32[]{:S(2)}) async-start(f32[16,128,1024]{2,1,0:T(8,128)} %bitcast.578), calls=%async_computation.5 | async-start | bytes 16777216 | tf_op jit(solution)/shard_map/all_to_all | solution.py:283
  593.8 1365.6 %all-gather.31.cloned.1.call-start = ((), (), s32[]{:S(2)}) async-start(), calls=%async_computation.16 | async-start | bytes 22282240 | tf_op jit(solution)/shard_map/all_gather | solution.py:319
  604.2 115.3 %collective-permute-start.8 = (bf16[512,1024]{1,0:T(8,128)(2,1)S(1)}, bf16[512,1024]{1,0:T(8,128)(2,1)S(1)}, u32[]{:S(2)}, u32[]{:S(2)}) collective-permute-start(bf16[512,1024]{1,0:T(8,128)(2,1)S(1)} %convert_element_type.660), channel_id=1, source_target_pairs={{0,2},{1,3},{2,0},{3,1},{4,6},{5,7},{6,4},{7,5},{8,10},{9,11},{10,... | collective-permute-start | bytes 3145736 | tf_op jit(solution)/shard_map/ppermute | solution.py:200
  605.9 138.7 %collective-permute-start.6 = (f32[2,256,1024]{2,1,0:T(8,128)}, f32[2,256,1024]{2,1,0:T(8,128)}, u32[]{:S(2)}, u32[]{:S(2)}) collective-permute-start(f32[2,256,1024]{2,1,0:T(8,128)} %dynamic-slice_bitcast_fusion.6), channel_id=1, source_target_pairs={{0,8},{1,9},{2,10},{3,11},{4,12},{5,13},{6,14},{7,15},{8,0},{9,1},... | collective-permute-start | bytes 6291464 | tf_op jit(solution)/shard_map/ppermute | solution.py:200
  642.3 100.6 %collective-permute-start.7 = (f32[2,64,1024]{2,1,0:T(8,128)}, f32[2,64,1024]{2,1,0:T(8,128)S(1)}, u32[]{:S(2)}, u32[]{:S(2)}) collective-permute-start(f32[2,64,1024]{2,1,0:T(8,128)} %dynamic-slice_bitcast_fusion.22), channel_id=1, source_target_pairs={{0,8},{1,9},{2,10},{3,11},{4,12},{5,13},{6,14},{7,15},{8,0},{9,1},... | collective-permute-start | bytes 1572872 | tf_op jit(solution)/shard_map/ppermute | solution.py:200
  642.7 101.0 %collective-permute-start.5 = (f32[2,64,1024]{2,1,0:T(8,128)}, f32[2,64,1024]{2,1,0:T(8,128)S(1)}, u32[]{:S(2)}, u32[]{:S(2)}) collective-permute-start(f32[2,64,1024]{2,1,0:T(8,128)} %dynamic-slice_bitcast_fusion.23), channel_id=1, source_target_pairs={{0,4},{1,5},{2,6},{3,7},{4,0},{5,1},{6,2},{7,3},{8,12},{9,13},{10,... | collective-permute-start | bytes 1572872 | tf_op jit(solution)/shard_map/ppermute | solution.py:200
  869.0 1106.5 %all-gather.23.cloned.1.call-start = ((), (), s32[]{:S(2)}) async-start(), calls=%async_computation.12 | async-start | bytes 22282240 | tf_op jit(solution)/shard_map/all_gather | solution.py:319
  963.2 225.0 %all-to-all-start.6 = ((f32[16,128,1024]{2,1,0:T(8,128)}), f32[16,128,1024]{2,1,0:T(8,128)}, u32[]{:S(2)}, u32[]{:S(2)}) async-start(f32[16,128,1024]{2,1,0:T(8,128)} %bitcast.573), calls=%async_computation.6 | async-start | bytes 16777216 | tf_op jit(solution)/shard_map/all_to_all | solution.py:306
  966.9 1026.7 %all-gather.29.cloned.1.call-start = ((), (), s32[]{:S(2)}) async-start(), calls=%async_computation.15 | async-start | bytes 22282240 | tf_op jit(solution)/shard_map/all_gather | solution.py:319
  992.3 129.7 %collective-permute-start.20 = (bf16[512,1024]{1,0:T(8,128)(2,1)S(1)}, bf16[512,1024]{1,0:T(8,128)(2,1)S(1)}, u32[]{:S(2)}, u32[]{:S(2)}) collective-permute-start(bf16[512,1024]{1,0:T(8,128)(2,1)S(1)} %convert_element_type.687), channel_id=1, source_target_pairs={{0,2},{1,3},{2,0},{3,1},{4,6},{5,7},{6,4},{7,5},{8,10},{9,11},{10,... | collective-permute-start | bytes 3145736 | tf_op jit(solution)/shard_map/ppermute | solution.py:200
  994.1 184.8 %collective-permute-start.18 = (f32[2,256,1024]{2,1,0:T(8,128)}, f32[2,256,1024]{2,1,0:T(8,128)}, u32[]{:S(2)}, u32[]{:S(2)}) collective-permute-start(f32[2,256,1024]{2,1,0:T(8,128)} %dynamic-slice_bitcast_fusion.4), channel_id=1, source_target_pairs={{0,8},{1,9},{2,10},{3,11},{4,12},{5,13},{6,14},{7,15},{8,0},{9,1},... | collective-permute-start | bytes 6291464 | tf_op jit(solution)/shard_map/ppermute | solution.py:200
  995.6 185.3 %collective-permute-start.16 = (f32[2,256,1024]{2,1,0:T(8,128)}, f32[2,256,1024]{2,1,0:T(8,128)}, u32[]{:S(2)}, u32[]{:S(2)}) collective-permute-start(f32[2,256,1024]{2,1,0:T(8,128)} %dynamic-slice_bitcast_fusion.5), channel_id=1, source_target_pairs={{0,4},{1,5},{2,6},{3,7},{4,0},{5,1},{6,2},{7,3},{8,12},{9,13},{10,... | collective-permute-start | bytes 6291464 | tf_op jit(solution)/shard_map/ppermute | solution.py:200
  1205.1 74.6 %collective-permute-start.26 = (f32[256,1024]{1,0:T(8,128)}, f32[256,1024]{1,0:T(8,128)}, u32[]{:S(2)}, u32[]{:S(2)}) collective-permute-start(f32[256,1024]{1,0:T(8,128)} %dynamic-slice_bitcast_fusion.12), channel_id=1, source_target_pairs={{0,4},{1,5},{2,6},{3,7},{4,0},{5,1},{6,2},{7,3},{8,12},{9,13},{10,... | collective-permute-start | bytes 3145736 | tf_op jit(solution)/shard_map/ppermute | solution.py:200
  1283.7 726.0 %all-gather.21.cloned.1.call-start = ((), (), s32[]{:S(2)}) async-start(), calls=%async_computation.11 | async-start | bytes 22282240 | tf_op jit(solution)/shard_map/all_gather | solution.py:319
  1286.8 262.0 %all-to-all-start.7 = ((f32[16,128,1024]{2,1,0:T(8,128)}), f32[16,128,1024]{2,1,0:T(8,128)}, u32[]{:S(2)}, u32[]{:S(2)}) async-start(f32[16,128,1024]{2,1,0:T(8,128)} %bitcast.574), calls=%async_computation.7 | async-start | bytes 16777216 | tf_op jit(solution)/shard_map/all_to_all | solution.py:306
  1290.3 736.8 %all-gather.27.cloned.1.call-start = ((), (), s32[]{:S(2)}) async-start(), calls=%async_computation.14 | async-start | bytes 22282240 | tf_op jit(solution)/shard_map/all_gather | solution.py:319
  1360.1 151.9 %collective-permute-start.35 = (bf16[2,1024,1024]{2,1,0:T(8,128)(2,1)S(1)}, bf16[2,1024,1024]{2,1,0:T(8,128)(2,1)S(1)}, u32[]{:S(2)}, u32[]{:S(2)}) collective-permute-start(bf16[2,1024,1024]{2,1,0:T(8,128)(2,1)S(1)} %pad_maximum_fusion.11), channel_id=1, source_target_pairs={{0,1},{1,0},{2,3},{3,2},{4,5},{5,4},{6,7},{7,6},{8,9},{9,8},{10,11... | collective-permute-start | bytes 12582920 | tf_op jit(solution)/shard_map/ppermute | solution.py:200
  1380.9 128.3 %collective-permute-start.32 = (bf16[512,1024]{1,0:T(8,128)(2,1)S(1)}, bf16[512,1024]{1,0:T(8,128)(2,1)S(1)}, u32[]{:S(2)}, u32[]{:S(2)}) collective-permute-start(bf16[512,1024]{1,0:T(8,128)(2,1)S(1)} %copy-done.11), channel_id=1, source_target_pairs={{0,2},{1,3},{2,0},{3,1},{4,6},{5,7},{6,4},{7,5},{8,10},{9,11},{10,... | collective-permute-start | bytes 3145736 | tf_op jit(solution)/shard_map/ppermute | solution.py:200
  1383.5 155.4 %collective-permute-start.30 = (f32[2,256,1024]{2,1,0:T(8,128)}, f32[2,256,1024]{2,1,0:T(8,128)}, u32[]{:S(2)}, u32[]{:S(2)}) collective-permute-start(f32[2,256,1024]{2,1,0:T(8,128)} %dynamic-slice_bitcast_fusion.2), channel_id=1, source_target_pairs={{0,8},{1,9},{2,10},{3,11},{4,12},{5,13},{6,14},{7,15},{8,0},{9,1},... | collective-permute-start | bytes 6291464 | tf_op jit(solution)/shard_map/ppermute | solution.py:200
  1383.5 158.3 %collective-permute-start.28 = (f32[2,256,1024]{2,1,0:T(8,128)}, f32[2,256,1024]{2,1,0:T(8,128)}, u32[]{:S(2)}, u32[]{:S(2)}) collective-permute-start(f32[2,256,1024]{2,1,0:T(8,128)} %dynamic-slice_bitcast_fusion.3), channel_id=1, source_target_pairs={{0,4},{1,5},{2,6},{3,7},{4,0},{5,1},{6,2},{7,3},{8,12},{9,13},{10,... | collective-permute-start | bytes 6291464 | tf_op jit(solution)/shard_map/ppermute | solution.py:200
  1569.3 74.6 %collective-permute-start.36 = (f32[256,1024]{1,0:T(8,128)}, f32[256,1024]{1,0:T(8,128)}, u32[]{:S(2)}, u32[]{:S(2)}) collective-permute-start(f32[256,1024]{1,0:T(8,128)} %dynamic-slice_bitcast_fusion.11), channel_id=1, source_target_pairs={{0,8},{1,9},{2,10},{3,11},{4,12},{5,13},{6,14},{7,15},{8,0},{9,1},... | collective-permute-start | bytes 3145736 | tf_op jit(solution)/shard_map/ppermute | solution.py:200
  1646.5 398.1 %all-gather.19.cloned.1.call-start = ((), (), s32[]{:S(2)}) async-start(), calls=%async_computation.10 | async-start | bytes 22282240 | tf_op jit(solution)/shard_map/all_gather | solution.py:319
  1647.7 223.9 %all-to-all-start.8 = ((f32[16,128,1024]{2,1,0:T(8,128)}), f32[16,128,1024]{2,1,0:T(8,128)}, u32[]{:S(2)}, u32[]{:S(2)}) async-start(f32[16,128,1024]{2,1,0:T(8,128)} %bitcast.575), calls=%async_computation.8 | async-start | bytes 16777216 | tf_op jit(solution)/shard_map/all_to_all | solution.py:306
  1651.4 419.1 %all-gather.25.cloned.1.call-start = ((), (), s32[]{:S(2)}) async-start(), calls=%async_computation.13 | async-start | bytes 22282240 | tf_op jit(solution)/shard_map/all_gather | solution.py:319
  1671.5 198.0 %collective-permute-start.42 = (f32[2,256,1024]{2,1,0:T(8,128)S(1)}, f32[2,256,1024]{2,1,0:T(8,128)S(1)}, u32[]{:S(2)}, u32[]{:S(2)}) collective-permute-start(f32[2,256,1024]{2,1,0:T(8,128)S(1)} %dynamic-slice_bitcast_fusion), channel_id=1, source_target_pairs={{0,8},{1,9},{2,10},{3,11},{4,12},{5,13},{6,14},{7,15},{8,0},{9,1},... | collective-permute-start | bytes 6291464 | tf_op jit(solution)/shard_map/ppermute | solution.py:200
  1673.3 198.0 %collective-permute-start.40 = (f32[2,256,1024]{2,1,0:T(8,128)S(1)}, f32[2,256,1024]{2,1,0:T(8,128)S(1)}, u32[]{:S(2)}, u32[]{:S(2)}) collective-permute-start(f32[2,256,1024]{2,1,0:T(8,128)S(1)} %dynamic-slice_bitcast_fusion.1), channel_id=1, source_target_pairs={{0,4},{1,5},{2,6},{3,7},{4,0},{5,1},{6,2},{7,3},{8,12},{9,13},{10,... | collective-permute-start | bytes 6291464 | tf_op jit(solution)/shard_map/ppermute | solution.py:200
  1674.8 190.1 %collective-permute-start.43 = (f32[2,64,1024]{2,1,0:T(8,128)S(1)}, f32[2,64,1024]{2,1,0:T(8,128)S(1)}, u32[]{:S(2)}, u32[]{:S(2)}) collective-permute-start(f32[2,64,1024]{2,1,0:T(8,128)S(1)} %dynamic-slice_bitcast_fusion.16), channel_id=1, source_target_pairs={{0,8},{1,9},{2,10},{3,11},{4,12},{5,13},{6,14},{7,15},{8,0},{9,1},... | collective-permute-start | bytes 1572872 | tf_op jit(solution)/shard_map/ppermute | solution.py:200
  1675.3 194.1 %collective-permute-start.41 = (f32[2,64,1024]{2,1,0:T(8,128)S(1)}, f32[2,64,1024]{2,1,0:T(8,128)S(1)}, u32[]{:S(2)}, u32[]{:S(2)}) collective-permute-start(f32[2,64,1024]{2,1,0:T(8,128)S(1)} %dynamic-slice_bitcast_fusion.17), channel_id=1, source_target_pairs={{0,4},{1,5},{2,6},{3,7},{4,0},{5,1},{6,2},{7,3},{8,12},{9,13},{10,... | collective-permute-start | bytes 1572872 | tf_op jit(solution)/shard_map/ppermute | solution.py:200
  1923.4 239.6 %all-gather.17.cloned.1.call-start = ((), (), s32[]{:S(2)}) async-start(), calls=%async_computation.9 | async-start | bytes 22282240 | tf_op jit(solution)/shard_map/all_gather | solution.py:319
  (169 other events, 4871.3 us)
Sparse Core Ops, SparseCore 0:
  869.1 181.9 all-gather.30
  1053.3 148.7 all-gather.22
  1283.8 221.0 all-gather.28
  1507.0 125.9 all-gather.20
  1646.6 222.6 all-gather.26
  1871.4 106.7 all-gather.18
  1980.4 90.0 all-gather.24
  2072.8 90.0 all-gather.16

commit v2 on v1

--- a/solution.py
+++ b/solution.py
@@ -8,6 +8,7 @@
 
 EPS = 1e-6
 CAP_DIV = 4
+TIER_DIV = 4
 CORE, X, Y, Z = 1, 2, 4, 8
 GROUP = 4
 
@@ -212,6 +213,16 @@
         dest_slot = owner_dev * cap_rows + slot_rank
         req_send = jnp.zeros((shards * cap_rows,), jnp.int32).at[dest_slot].set(local_row)
         req_recv = lax.all_to_all(req_send, "emb", 0, 0, tiled=True)
+        tier_rows = cap_rows // TIER_DIV
+        spilled = slot_rank >= tier_rows
+        spill_rank = jnp.cumsum(spilled.astype(jnp.int32)) - 1
+        tier_slot = jnp.where(spilled, shards * tier_rows + spill_rank, owner_dev * tier_rows + slot_rank)
+        spill_ids = jnp.full((shards * tier_rows + cap_rows,), -1, jnp.int32).at[tier_slot].set(tok_ids)[shards * tier_rows:]
+        spill_info = lax.all_gather(jnp.stack([spill_ids, jnp.full((cap_rows,), 1, jnp.int32) * (spill_rank[-1] + 1)]), "emb")
+        req_recv, spill_info = lax.optimization_barrier((req_recv, spill_info))
+        fits = jnp.max(spill_info[:, 1]) <= cap_rows
+        spill_row = spill_info[:, 0].reshape(-1) - me * rows_dev
+        spill_row = jnp.where((spill_row >= 0) & (spill_row < rows_dev), spill_row, rows_dev)
         sync = lax.optimization_barrier
         blocks = shards // GROUP
 
@@ -243,11 +254,6 @@
             pick = (jnp.arange(GROUP) == quarter)[:, None]
             return jnp.sum(jnp.where(pick, cut, 0), axis=-2).reshape(arr.shape[:-1] + (wide // GROUP,))
 
-        def dx_step(layer, d_x):
-            g_out = d_x.astype(jnp.bfloat16)
-            d_x, d_rows = layer_bwd(d_x, g_out, saved_list[layer], rows_list[layer], w_up[layer], w_down[layer], w_gate[layer], w_proj[layer], layer > 0)
-            return d_x, jnp.zeros((shards * cap_rows, emb_dim), jnp.float32).at[dest_slot].set(d_rows)
-
         def grads_head(layer, ue, o_rows):
             u_rows, e_part = ue[0], side_cols(ue[1])
             h_pre = dot32("nd,df->nf", u_rows, up_q[layer]).astype(jnp.bfloat16)
@@ -272,56 +278,84 @@
         def sum_with(mine, sent, bits):
             return [own + swap(arr, bit) for own, arr, bit in zip(mine, sent, bits)]
 
-        outs = blank([w_up.shape, w_gate.shape, w_down.shape, w_proj.shape, ple_tables.shape])
-        col_outs, row_outs, table_out = (outs[0], outs[1]), (outs[2], outs[3]), outs[4]
         up_q, down_q, proj_q = weight_slices(quarter[None], w_up, w_gate, w_down, w_proj, blocks)
         gate_q = side_cols(w_gate)
-        d_x = d_out.astype(jnp.float32)
-        ue_last = group(acts_list[last])
-        d_x, slots = dx_step(last, d_x)
-        d_x, slots, ue_last, o_last = sync((d_x, slots, ue_last, o_last))
-        recv = lax.all_to_all(slots, "emb", 0, 0, tiled=True)
-        grads = grads_tail(*grads_head(last, ue_last, o_last))
-        gathered = {}
-        way1, way2 = (Y, Y, Z, Z), (Z, Z, Y, Y)
-        pos1, pos2 = (y_pos, y_pos, z_pos, z_pos), (z_pos, z_pos, y_pos, y_pos)
-        not1, not2 = [1 - p for p in pos1], [1 - p for p in pos2]
-        for layer in reversed(range(layers)):
-            sent = take(grads, not1, (1, 1, 0, 0))
-            sent, grads, d_x = sync((sent, grads, d_x))
-            sums = sum_with(take(grads, pos1, (1, 1, 0, 0)), sent, way1)
-            if layer > 0:
-                o_next = group(d_x.astype(jnp.bfloat16))
-                ue_next = group(acts_list[layer - 1])
-                d_x, slots = dx_step(layer - 1, d_x)
-                sums, d_x, slots, o_next, ue_next, recv = sync((sums, d_x, slots, o_next, ue_next, recv))
+
+        def backward(tiered):
+            if tiered:
+                slot_of, n_slots = tier_slot, shards * tier_rows + cap_rows
+                base_row = req_recv.reshape(shards, cap_rows)[:, :tier_rows].reshape(-1)
+                row_of = jnp.concatenate([base_row, spill_row])
             else:
-                sums, recv = sync((sums, recv))
-            sent = take(sums, not2, (0, 0, 0, 0))
-            sent, sums = sync((sent, sums))
-            sums = sum_with(take(sums, pos2, (0, 0, 0, 0)), sent, way2)
-            table = jax.ops.segment_sum(recv, req_recv, num_segments=rows_dev)
-            table_out = place_table(layer, table, table_out)
-            if layer > 0:
-                recv = lax.all_to_all(slots, "emb", 0, 0, tiled=True)
-                head = grads_head(layer - 1, ue_next, o_next)
-                sums, head, table_out = sync((sums, head, table_out))
-            else:
-                sums = sync(sums)
-            cols_piece = jnp.concatenate(sums[:2], axis=0)
-            rows_piece = jnp.concatenate(sums[2:], axis=0)
-            if layer + 2 in gathered:
-                ready = gathered.pop(layer + 2)
-                col_outs = place_cols(layer + 2, ready[0], *col_outs)
-                row_outs = place_rows(layer + 2, ready[1], *row_outs)
-            if layer > 0:
-                grads = grads_tail(*head)
-            gathered[layer] = (lax.all_gather(cols_piece, "emb"), lax.all_gather(rows_piece, "emb"))
-        for layer in sorted(gathered, reverse=True):
-            cols_all, rows_all = gathered[layer]
-            col_outs = place_cols(layer, cols_all, *col_outs)
-            row_outs = place_rows(layer, rows_all, *row_outs)
-        return (x_out, table_out, col_outs[0], row_outs[0], col_outs[1], row_outs[1])
+                slot_of, n_slots, row_of = dest_slot, shards * cap_rows, req_recv
+
+            def to_slots(d_rows):
+                return jnp.zeros((n_slots, emb_dim), jnp.float32).at[slot_of].set(d_rows)
+
+            def exchange(slots):
+                if not tiered:
+                    return (lax.all_to_all(slots, "emb", 0, 0, tiled=True),)
+                cut = shards * tier_rows
+                near = lax.all_to_all(slots[:cut], "emb", 0, 0, tiled=True)
+                return near, lax.all_gather(slots[cut:], "emb", tiled=True)
+
+            def add_rows(parts):
+                return jax.ops.segment_sum(jnp.concatenate(parts, axis=0), row_of, num_segments=rows_dev)
+
+            def dx_step(layer, d_x):
+                g_out = d_x.astype(jnp.bfloat16)
+                d_x, d_rows = layer_bwd(d_x, g_out, saved_list[layer], rows_list[layer], w_up[layer], w_down[layer], w_gate[layer], w_proj[layer], layer > 0)
+                return d_x, to_slots(d_rows)
+
+            outs = blank([w_up.shape, w_gate.shape, w_down.shape, w_proj.shape, ple_tables.shape])
+            col_outs, row_outs, table_out = (outs[0], outs[1]), (outs[2], outs[3]), outs[4]
+            d_x = d_out.astype(jnp.float32)
+            ue_last = group(acts_list[last])
+            d_x, slots = dx_step(last, d_x)
+            d_x, slots, ue_last, o_first = sync((d_x, slots, ue_last, o_last))
+            arrived = {last: exchange(slots)}
+            grads = grads_tail(*grads_head(last, ue_last, o_first))
+            gathered = {}
+            way1, way2 = (Y, Y, Z, Z), (Z, Z, Y, Y)
+            pos1, pos2 = (y_pos, y_pos, z_pos, z_pos), (z_pos, z_pos, y_pos, y_pos)
+            not1, not2 = [1 - p for p in pos1], [1 - p for p in pos2]
+            for layer in reversed(range(layers)):
+                sent = take(grads, not1, (1, 1, 0, 0))
+                sent, grads, d_x = sync((sent, grads, d_x))
+                sums = sum_with(take(grads, pos1, (1, 1, 0, 0)), sent, way1)
+                if layer > 0:
+                    o_next = group(d_x.astype(jnp.bfloat16))
+                    ue_next = group(acts_list[layer - 1])
+                    d_x, slots = dx_step(layer - 1, d_x)
+                    sums, d_x, slots, o_next, ue_next, table_out = sync((sums, d_x, slots, o_next, ue_next, table_out))
+                else:
+                    sums = sync(sums)
+                sent = take(sums, not2, (0, 0, 0, 0))
+                sent, sums = sync((sent, sums))
+                sums = sum_with(take(sums, pos2, (0, 0, 0, 0)), sent, way2)
+                if layer > 0:
+                    arrived[layer - 1] = exchange(slots)
+                    head = grads_head(layer - 1, ue_next, o_next)
+                    sums, head, arrived[layer], table_out = sync((sums, head, arrived[layer], table_out))
+                else:
+                    sums, arrived[layer] = sync((sums, arrived[layer]))
+                table_out = place_table(layer, add_rows(arrived[layer]), table_out)
+                cols_piece = jnp.concatenate(sums[:2], axis=0)
+                rows_piece = jnp.concatenate(sums[2:], axis=0)
+                if layer + 2 in gathered:
+                    ready = gathered.pop(layer + 2)
+                    col_outs = place_cols(layer + 2, ready[0], *col_outs)
+                    row_outs = place_rows(layer + 2, ready[1], *row_outs)
+                if layer > 0:
+                    grads = grads_tail(*head)
+                gathered[layer] = (lax.all_gather(cols_piece, "emb"), lax.all_gather(rows_piece, "emb"))
+            for layer in sorted(gathered, reverse=True):
+                cols_all, rows_all = gathered[layer]
+                col_outs = place_cols(layer, cols_all, *col_outs)
+                row_outs = place_rows(layer, rows_all, *row_outs)
+            return (table_out, col_outs[0], row_outs[0], col_outs[1], row_outs[1])
+
+        return (x_out,) + lax.cond(fits, lambda: backward(True), lambda: backward(False))
 
     return jax.shard_map(
         device_step,

time: 2200 us -> 2130 us (0.968)
  waiting for transfers between devices: 1020 us -> 831 us
  blocking collectives: 0 us -> 65 us
  other arithmetic: 279 us -> 332 us
    ppermute x48, waiting for transfers between devices: 888 us -> 361 us  [swap(): lax.ppermute(arr, 'emb', [(dev, dev ^ axis_bit) for dev in range(shards)])]
    all_gather x8 -> x12, waiting for transfers between devices: 84.5 us -> 409 us  [the longest x4 224 us: backward(): lax.all_gather(rows_piece, 'emb')]
    all_to_all x0 -> x1, blocking collectives: none -> 52 us  [device_step(): returned = lax.all_to_all(served, 'emb', 0, 0, tiled=True)]
    slice x8 -> x5, local copies, waits for them, and re-layouts: 46.9 us -> 27.9 us  [grads_head(): u_rows, e_part = (ue[0], side_cols(ue[1]))]
    all_to_all x4 -> x3, waiting for transfers between devices: 49.9 us -> 60.9 us  [device_step(): returned = lax.all_to_all(served, 'emb', 0, 0, tiled=True)]
  transfers between devices with their start and end apart: 65 -> 68, of which waited for: 23 -> 22; matrix products, arithmetic and copies ran while one was open for 31% -> 35% of each run, Pallas kernels for 8% -> 8%
where the time goes in v2:
time: 2130 us; the launch traced here: 2120 us
  waiting for transfers between devices  831 us (39%)
  matrix products  370 us (17%)
  other arithmetic  332 us (16%)
  local copies, waits for them, and re-layouts  224 us (11%)
  Pallas kernels  196 us (9%)
  starting transfers between devices  78.2 us (4%)
  blocking collectives  65 us (3%)
    dot_general x57, matrix products, dot32(): return jnp.einsum(spec, a, b, preferred_element_type=jnp.float32)  370 us
    ppermute x48, waiting for transfers between devices, swap(): lax.ppermute(arr, 'emb', [(dev, dev ^ axis_bit) for dev in range(shards)])  361 us
    all_gather x4, waiting for transfers between devices, backward(): lax.all_gather(rows_piece, 'emb')  224 us
    all_gather x4, waiting for transfers between devices, backward(): lax.all_gather(cols_piece, 'emb')  185 us
    scatter-add x4, other arithmetic, add_rows(): jax.ops.segment_sum(jnp.concatenate(parts, axis=0), row_of, num_segments=...  114 us
    pallas_call x4, Pallas kernels, place_cols(): pl.pallas_call(body, grid=(n // at_once,), in_specs=[pl.BlockSpec((at_onc...  70.9 us
    pallas_call x4, Pallas kernels, place_rows(): pl.pallas_call(body, grid=(n // at_once,), in_specs=[pl.BlockSpec((at_onc...  65.2 us
    all_to_all x3, waiting for transfers between devices, device_step(): returned = lax.all_to_all(served, 'emb', 0, 0, tiled=True)  60.9 us
  transfers between devices with their start and end apart: 68, of which 22 were waited for; matrix products, arithmetic and copies ran while one was open for 35% of the time, Pallas kernels for 8%

profile of v2, /device:TPU:0, one launch (start us, length us, event | category | flops | bytes accessed | tf_op | source)
XLA Modules:
  0.0 2121.5 jit_solution(11004685880617251767)
XLA Ops:
  22.7 18.0 slice_bitcast_fusion.34
  123.7 52.0 %all_to_all.132 = bf16[16,128,1024]{2,1,0:T(8,128)(2,1)} all-to-all(bf16[16,128,1024]{2,1,0:T(8,128)(2,1)S(1)} %bitcast.1143), channel_id=1, replica_groups=mesh['emb'=16] {'emb'}, dimensions={0} | all-to-all | bytes 8388608 | tf_op jit(solution)/shard_map/all_to_all | solution.py:241
  180.9 50.6 %all-to-all-done.12 = bf16[16,128,1024]{2,1,0:T(8,128)(2,1)} async-done(((bf16[16,128,1024]{2,1,0:T(8,128)(2,1)}), bf16[16,128,1024]{2,1,0:T(8,128)(2,1)}, u32[]{:S(2)}, u32[]{:S(2)}) %all-to-all-start.12) | async-done | bytes 4194336 | tf_op jit(solution)/shard_map/all_to_all | solution.py:241
  248.7 18.4 weight_slices.1
  446.0 1668.3 %conditional.1 = (f32[4,3144,1024]{2,1,0:T(8,128)}, f32[4,1024,4096]{2,1,0:T(8,128)}, f32[4,4096,1024]{2,1,0:T(8,128)}, f32[4,1024,1024]{2,1,0:T(8,128)}, f32[4,1024,1024]{2,1,0:T(8,128)}) conditional(s32[]{:T(128)} %convert_element_type.1064, (s32[2048]{0:T(1024)S(1)}, bf16[512,1024]{1,0:T(8,128)(2,1)S(1)}, f32[512,1]{0,1:T(1,128)S(1)}, ...), branch_computations={%region_13.31_spmd, %region_29.47_spmd} | conditional | flops 120436572160 | bytes 3267904512 | solution.py:358
  475.7 27.4 %collective-permute-done.46 = bf16[2,512,1024]{2,1,0:T(8,128)(2,1)} collective-permute-done((bf16[2,512,1024]{2,1,0:T(8,128)(2,1)S(1)}, bf16[2,512,1024]{2,1,0:T(8,128)(2,1)}, u32[]{:S(2)}, u32[]{:S(2)}) %collective-permute-start.46) | collective-permute-done | bytes 2097184 | tf_op jit(solution)/shard_map/cond/branch_1_fun/ppermute | solution.py:201
  507.2 17.6 multiply_reduce_fusion.5
  552.3 40.0 %collective-permute-done.66 = bf16[2,512,1024]{1,2,0:T(8,128)(2,1)} collective-permute-done((bf16[2,512,1024]{1,2,0:T(8,128)(2,1)}, bf16[2,512,1024]{1,2,0:T(8,128)(2,1)}, u32[]{:S(2)}, u32[]{:S(2)}) %collective-permute-start.66) | collective-permute-done | bytes 2097184 | tf_op jit(solution)/shard_map/cond/branch_1_fun/ppermute | solution.py:201
  686.0 17.0 multiply_reduce_fusion.4
  875.8 17.0 multiply_reduce_fusion.3
  898.1 28.6 %scatter_custom_fusion.11.table_ref = f32[3144,1024]{1,0:T(8,128)} fusion(s32[2560]{0:T(1024)} %pad_add_fusion, f32[2048,1024]{1,0:T(8,128)} %all-gather.55.cloned.1.call-done, f32[]{:T(128)} %constant.565, f32[512,1024]{1,0:T(8,128)} %bitcast.212, f32[]{:T(128)} %constant.500.clone), kind=kCustom, calls=%fused_computation.655 | custom fusion | flops 5242880 | bytes 23364608 | tf_op jit(solution)/shard_map/cond/branch_1_fun/scatter-add | solution.py:303
  956.8 44.9 %collective-permute-done.78 = bf16[2,512,1024]{1,2,0:T(8,128)(2,1)} collective-permute-done((bf16[2,512,1024]{1,2,0:T(8,128)(2,1)}, bf16[2,512,1024]{1,2,0:T(8,128)(2,1)}, u32[]{:S(2)}, u32[]{:S(2)}) %collective-permute-start.78) | collective-permute-done | bytes 2097184 | tf_op jit(solution)/shard_map/cond/branch_1_fun/ppermute | solution.py:201
  1094.0 20.9 collective-permute-done.76
  1135.2 28.6 %scatter_custom_fusion.13.table_ref = f32[3144,1024]{1,0:T(8,128)} fusion(s32[2560]{0:T(1024)} %pad_add_fusion, f32[2048,1024]{1,0:T(8,128)} %all-gather.57.cloned.1.call-done, f32[]{:T(128)} %constant.565, f32[512,1024]{1,0:T(8,128)} %bitcast.248, f32[]{:T(128)} %constant.500.clone), kind=kCustom, calls=%fused_computation.659 | custom fusion | flops 5242880 | bytes 23364608 | tf_op jit(solution)/shard_map/cond/branch_1_fun/scatter-add | solution.py:303
  1251.5 29.8 %collective-permute-done.80 = f32[256,1024]{1,0:T(8,128)S(1)} collective-permute-done((f32[256,1024]{1,0:T(8,128)S(1)}, f32[256,1024]{1,0:T(8,128)S(1)}, u32[]{:S(2)}, u32[]{:S(2)}) %collective-permute-start.80) | collective-permute-done | bytes 1048608 | tf_op jit(solution)/shard_map/cond/branch_1_fun/ppermute | solution.py:201
  1318.5 111.9 %collective-permute-done.85 = f32[2,64,1024]{2,1,0:T(8,128)} collective-permute-done((f32[2,64,1024]{2,1,0:T(8,128)}, f32[2,64,1024]{2,1,0:T(8,128)}, u32[]{:S(2)}, u32[]{:S(2)}) %collective-permute-start.85) | collective-permute-done | bytes 524320 | tf_op jit(solution)/shard_map/cond/branch_1_fun/ppermute | solution.py:201
  1442.3 43.6 %collective-permute-done.89 = f32[64,1024]{1,0:T(8,128)S(1)} collective-permute-done((f32[64,1024]{1,0:T(8,128)S(1)}, f32[64,1024]{1,0:T(8,128)S(1)}, u32[]{:S(2)}, u32[]{:S(2)}) %collective-permute-start.89) | collective-permute-done | bytes 262176 | tf_op jit(solution)/shard_map/cond/branch_1_fun/ppermute | solution.py:201
  1492.4 27.7 %scatter_custom_fusion.15.table_ref = f32[3144,1024]{1,0:T(8,128)} fusion(s32[2560]{0:T(1024)} %pad_add_fusion, f32[2048,1024]{1,0:T(8,128)} %all-gather.59.cloned.1.call-done, f32[]{:T(128)} %constant.565, f32[512,1024]{1,0:T(8,128)S(1)} %bitcast.1152, f32[]{:T(128)} %constant.500.clone), kind=kCustom, calls=%fused_computation.667 | custom fusion | flops 5242880 | bytes 23364608 | tf_op jit(solution)/shard_map/cond/branch_1_fun/scatter-add | solution.py:303
  1530.4 28.8 %scatter_custom_fusion.14.table_ref = f32[3144,1024]{1,0:T(8,128)} fusion(s32[2560]{0:T(1024)} %pad_add_fusion, f32[2048,1024]{1,0:T(8,128)} %all-gather.61.cloned.1.call-done, f32[]{:T(128)} %constant.565, f32[512,1024]{1,0:T(8,128)} %bitcast.301, f32[]{:T(128)} %constant.500.clone), kind=kCustom, calls=%fused_computation.663 | custom fusion | flops 5242880 | bytes 23364608 | tf_op jit(solution)/shard_map/cond/branch_1_fun/scatter-add | solution.py:303
  1569.5 17.7 place_cols.12
  1587.2 16.6 place_rows.12
  1603.8 32.6 %all-gather.67.cloned.1.call-done = f32[5120,1024]{1,0:T(8,128)} async-done(((f32[320,1024]{1,0:T(8,128)}), f32[5120,1024]{1,0:T(8,128)}) %all-gather.67.cloned.1.call-update) | async-done | bytes 20971536 | tf_op jit(solution)/shard_map/cond/branch_1_fun/all_gather | solution.py:351
  1636.5 17.7 place_cols.13
  1654.2 74.6 %all-gather.75.cloned.1.call-done = f32[5120,1024]{1,0:T(8,128)} async-done(((f32[320,1024]{1,0:T(8,128)}), f32[5120,1024]{1,0:T(8,128)}) %all-gather.75.cloned.1.call-update) | async-done | bytes 20971536 | tf_op jit(solution)/shard_map/cond/branch_1_fun/all_gather | solution.py:351
  1728.9 16.3 place_rows.13
  1745.1 76.1 %all-gather.65.cloned.1.call-done = f32[5120,1024]{1,0:T(8,128)} async-done(((f32[320,1024]{1,0:T(8,128)}), f32[5120,1024]{1,0:T(8,128)}) %all-gather.65.cloned.1.call-update) | async-done | bytes 20971536 | tf_op jit(solution)/shard_map/cond/branch_1_fun/all_gather | solution.py:351
  1821.2 17.7 place_cols.14
  1839.0 74.5 %all-gather.73.cloned.1.call-done = f32[5120,1024]{1,0:T(8,128)} async-done(((f32[320,1024]{1,0:T(8,128)}), f32[5120,1024]{1,0:T(8,128)}) %all-gather.73.cloned.1.call-update) | async-done | bytes 20971536 | tf_op jit(solution)/shard_map/cond/branch_1_fun/all_gather | solution.py:351
  1913.5 16.3 place_rows.14
  1929.7 76.1 %all-gather.63.cloned.1.call-done = f32[5120,1024]{1,0:T(8,128)} async-done(((f32[320,1024]{1,0:T(8,128)}), f32[5120,1024]{1,0:T(8,128)}) %all-gather.63.cloned.1.call-update) | async-done | bytes 20971536 | tf_op jit(solution)/shard_map/cond/branch_1_fun/all_gather | solution.py:351
  2005.8 17.7 place_cols.15
  2023.6 74.5 %all-gather.71.cloned.1.call-done = f32[5120,1024]{1,0:T(8,128)} async-done(((f32[320,1024]{1,0:T(8,128)}), f32[5120,1024]{1,0:T(8,128)}) %all-gather.71.cloned.1.call-update) | async-done | bytes 20971536 | tf_op jit(solution)/shard_map/cond/branch_1_fun/all_gather | solution.py:351
  (599 shorter events, 944.3 us)
Async XLA Ops:
  179.2 96.0 %collective-permute-start.92 = (bf16[512,1024]{1,0:T(8,128)(2,1)S(1)}, bf16[512,1024]{1,0:T(8,128)(2,1)S(1)}, u32[]{:S(2)}, u32[]{:S(2)}) collective-permute-start(bf16[512,1024]{1,0:T(8,128)(2,1)S(1)} %copy-done.18), channel_id=1, source_target_pairs={{0,2},{1,3},{2,0},{3,1},{4,6},{5,7},{6,4},{7,5},{8,10},{9,11},{10,... | collective-permute-start | bytes 3145736 | tf_op jit(solution)/shard_map/ppermute | solution.py:201
  454.0 372.1 %all-gather.55.cloned.1.call-start = ((), (), s32[]{:S(2)}) async-start(), calls=%async_computation.21 | async-start | bytes 8912896 | tf_op jit(solution)/shard_map/cond/branch_1_fun/all_gather | solution.py:300
  460.5 87.6 %collective-permute-start.54 = (bf16[2,512,1024]{1,2,0:T(8,128)(2,1)}, bf16[2,512,1024]{1,2,0:T(8,128)(2,1)}, u32[]{:S(2)}, u32[]{:S(2)}) collective-permute-start(bf16[2,512,1024]{1,2,0:T(8,128)(2,1)} %copy.148), channel_id=1, source_target_pairs={{0,2},{1,3},{2,0},{3,1},{4,6},{5,7},{6,4},{7,5},{8,10},{9,11},{10,... | collective-permute-start | bytes 6291464 | tf_op jit(solution)/shard_map/cond/branch_1_fun/ppermute | solution.py:201
  464.5 127.8 %collective-permute-start.66 = (bf16[2,512,1024]{1,2,0:T(8,128)(2,1)}, bf16[2,512,1024]{1,2,0:T(8,128)(2,1)}, u32[]{:S(2)}, u32[]{:S(2)}) collective-permute-start(bf16[2,512,1024]{1,2,0:T(8,128)(2,1)} %copy.149), channel_id=1, source_target_pairs={{0,2},{1,3},{2,0},{3,1},{4,6},{5,7},{6,4},{7,5},{8,10},{9,11},{10,... | collective-permute-start | bytes 6291464 | tf_op jit(solution)/shard_map/cond/branch_1_fun/ppermute | solution.py:201
  507.2 89.3 %collective-permute-start.47 = (bf16[2,1024,1024]{2,1,0:T(8,128)(2,1)}, bf16[2,1024,1024]{2,1,0:T(8,128)(2,1)}, u32[]{:S(2)}, u32[]{:S(2)}) collective-permute-start(bf16[2,1024,1024]{2,1,0:T(8,128)(2,1)} %pad_maximum_fusion.26), channel_id=1, source_target_pairs={{0,1},{1,0},{2,3},{3,2},{4,5},{5,4},{6,7},{7,6},{8,9},{9,8},{10,11... | collective-permute-start | bytes 12582920 | tf_op jit(solution)/shard_map/cond/branch_1_fun/ppermute | solution.py:201
  552.3 150.8 %collective-permute-start.55 = (bf16[2,1024,1024]{1,2,0:T(8,128)(2,1)}, bf16[2,1024,1024]{1,2,0:T(8,128)(2,1)}, u32[]{:S(2)}, u32[]{:S(2)}) collective-permute-start(bf16[2,1024,1024]{1,2,0:T(8,128)(2,1)} %pad_maximum_fusion.28), channel_id=1, source_target_pairs={{0,1},{1,0},{2,3},{3,2},{4,5},{5,4},{6,7},{7,6},{8,9},{9,8},{10,11... | collective-permute-start | bytes 12582920 | tf_op jit(solution)/shard_map/cond/branch_1_fun/ppermute | solution.py:201
  596.5 117.7 %collective-permute-start.67 = (bf16[2,1024,1024]{1,2,0:T(8,128)(2,1)}, bf16[2,1024,1024]{1,2,0:T(8,128)(2,1)}, u32[]{:S(2)}, u32[]{:S(2)}) collective-permute-start(bf16[2,1024,1024]{1,2,0:T(8,128)(2,1)} %pad_maximum_fusion.30), channel_id=1, source_target_pairs={{0,1},{1,0},{2,3},{3,2},{4,5},{5,4},{6,7},{7,6},{8,9},{9,8},{10,11... | collective-permute-start | bytes 12582920 | tf_op jit(solution)/shard_map/cond/branch_1_fun/ppermute | solution.py:201
  608.2 218.0 %all-to-all-start.4 = ((f32[16,32,1024]{2,1,0:T(8,128)}), f32[16,32,1024]{2,1,0:T(8,128)}, u32[]{:S(2)}, u32[]{:S(2)}) async-start(f32[16,32,1024]{2,1,0:T(8,128)} %bitcast.211), calls=%async_computation.4 | async-start | bytes 4194304 | tf_op jit(solution)/shard_map/cond/branch_1_fun/all_to_all | solution.py:299
  611.5 455.6 %all-gather.57.cloned.1.call-start = ((), (), s32[]{:S(2)}) async-start(), calls=%async_computation.22 | async-start | bytes 8912896 | tf_op jit(solution)/shard_map/cond/branch_1_fun/all_gather | solution.py:300
  781.7 500.9 %all-gather.59.cloned.1.call-start = ((), (), s32[]{:S(2)}) async-start(), calls=%async_computation.23 | async-start | bytes 8912896 | tf_op jit(solution)/shard_map/cond/branch_1_fun/all_gather | solution.py:300
  849.6 91.2 %collective-permute-start.61 = (f32[2,64,1024]{2,1,0:T(8,128)}, f32[2,64,1024]{2,1,0:T(8,128)}, u32[]{:S(2)}, u32[]{:S(2)}) collective-permute-start(f32[2,64,1024]{2,1,0:T(8,128)} %dynamic-slice_bitcast_fusion.53), channel_id=1, source_target_pairs={{0,4},{1,5},{2,6},{3,7},{4,0},{5,1},{6,2},{7,3},{8,12},{9,13},{10,... | collective-permute-start | bytes 1572872 | tf_op jit(solution)/shard_map/cond/branch_1_fun/ppermute | solution.py:201
  851.0 92.3 %collective-permute-start.63 = (f32[2,64,1024]{2,1,0:T(8,128)}, f32[2,64,1024]{2,1,0:T(8,128)}, u32[]{:S(2)}, u32[]{:S(2)}) collective-permute-start(f32[2,64,1024]{2,1,0:T(8,128)} %dynamic-slice_bitcast_fusion.52), channel_id=1, source_target_pairs={{0,8},{1,9},{2,10},{3,11},{4,12},{5,13},{6,14},{7,15},{8,0},{9,1},... | collective-permute-start | bytes 1572872 | tf_op jit(solution)/shard_map/cond/branch_1_fun/ppermute | solution.py:201
  852.7 92.7 %collective-permute-start.60 = (f32[2,256,1024]{2,1,0:T(8,128)}, f32[2,256,1024]{2,1,0:T(8,128)}, u32[]{:S(2)}, u32[]{:S(2)}) collective-permute-start(f32[2,256,1024]{2,1,0:T(8,128)} %dynamic-slice_bitcast_fusion.37), channel_id=1, source_target_pairs={{0,4},{1,5},{2,6},{3,7},{4,0},{5,1},{6,2},{7,3},{8,12},{9,13},{10,... | collective-permute-start | bytes 6291464 | tf_op jit(solution)/shard_map/cond/branch_1_fun/ppermute | solution.py:201
  853.7 95.0 %collective-permute-start.62 = (f32[2,256,1024]{2,1,0:T(8,128)}, f32[2,256,1024]{2,1,0:T(8,128)}, u32[]{:S(2)}, u32[]{:S(2)}) collective-permute-start(f32[2,256,1024]{2,1,0:T(8,128)} %dynamic-slice_bitcast_fusion.36), channel_id=1, source_target_pairs={{0,8},{1,9},{2,10},{3,11},{4,12},{5,13},{6,14},{7,15},{8,0},{9,1},... | collective-permute-start | bytes 6291464 | tf_op jit(solution)/shard_map/cond/branch_1_fun/ppermute | solution.py:201
  1006.5 112.4 %collective-permute-start.79 = (bf16[2,1024,1024]{1,2,0:T(8,128)(2,1)}, bf16[2,1024,1024]{1,2,0:T(8,128)(2,1)}, u32[]{:S(2)}, u32[]{:S(2)}) collective-permute-start(bf16[2,1024,1024]{1,2,0:T(8,128)(2,1)} %pad_maximum_fusion.32), channel_id=1, source_target_pairs={{0,1},{1,0},{2,3},{3,2},{4,5},{5,4},{6,7},{7,6},{8,9},{9,8},{10,11... | collective-permute-start | bytes 12582920 | tf_op jit(solution)/shard_map/cond/branch_1_fun/ppermute | solution.py:201
  1011.3 477.1 %all-gather.61.cloned.1.call-start = ((), (), s32[]{:S(2)}) async-start(), calls=%async_computation.24 | async-start | bytes 8912896 | tf_op jit(solution)/shard_map/cond/branch_1_fun/all_gather | solution.py:300
  1091.7 86.0 %collective-permute-start.72 = (f32[2,256,1024]{2,1,0:T(8,128)}, f32[2,256,1024]{2,1,0:T(8,128)}, u32[]{:S(2)}, u32[]{:S(2)}) collective-permute-start(f32[2,256,1024]{2,1,0:T(8,128)} %dynamic-slice_bitcast_fusion.35), channel_id=1, source_target_pairs={{0,4},{1,5},{2,6},{3,7},{4,0},{5,1},{6,2},{7,3},{8,12},{9,13},{10,... | collective-permute-start | bytes 6291464 | tf_op jit(solution)/shard_map/cond/branch_1_fun/ppermute | solution.py:201
  1093.2 88.6 %collective-permute-start.74 = (f32[2,256,1024]{2,1,0:T(8,128)}, f32[2,256,1024]{2,1,0:T(8,128)}, u32[]{:S(2)}, u32[]{:S(2)}) collective-permute-start(f32[2,256,1024]{2,1,0:T(8,128)} %dynamic-slice_bitcast_fusion.34), channel_id=1, source_target_pairs={{0,8},{1,9},{2,10},{3,11},{4,12},{5,13},{6,14},{7,15},{8,0},{9,1},... | collective-permute-start | bytes 6291464 | tf_op jit(solution)/shard_map/cond/branch_1_fun/ppermute | solution.py:201
  1190.8 378.8 %all-gather.69.cloned.1.call-start = ((), (), s32[]{:S(2)}) async-start(), calls=%async_computation.28 | async-start | bytes 22282240 | tf_op jit(solution)/shard_map/cond/branch_1_fun/all_gather | solution.py:351
  1193.4 393.8 %all-gather.77.cloned.1.call-start = ((), (), s32[]{:S(2)}) async-start(), calls=%async_computation.32 | async-start | bytes 22282240 | tf_op jit(solution)/shard_map/cond/branch_1_fun/all_gather | solution.py:351
  1195.9 440.6 %all-gather.67.cloned.1.call-start = ((), (), s32[]{:S(2)}) async-start(), calls=%async_computation.27 | async-start | bytes 22282240 | tf_op jit(solution)/shard_map/cond/branch_1_fun/all_gather | solution.py:351
  1198.6 530.2 %all-gather.75.cloned.1.call-start = ((), (), s32[]{:S(2)}) async-start(), calls=%async_computation.31 | async-start | bytes 22282240 | tf_op jit(solution)/shard_map/cond/branch_1_fun/all_gather | solution.py:351
  1202.6 80.0 %all-to-all-start.6 = ((f32[16,32,1024]{2,1,0:T(8,128)}), f32[16,32,1024]{2,1,0:T(8,128)S(1)}, u32[]{:S(2)}, u32[]{:S(2)}) async-start(f32[16,32,1024]{2,1,0:T(8,128)} %bitcast.1154), calls=%async_computation.6 | async-start | bytes 4194304 | tf_op jit(solution)/shard_map/cond/branch_1_fun/all_to_all | solution.py:299
  1205.2 616.0 %all-gather.65.cloned.1.call-start = ((), (), s32[]{:S(2)}) async-start(), calls=%async_computation.26 | async-start | bytes 22282240 | tf_op jit(solution)/shard_map/cond/branch_1_fun/all_gather | solution.py:351
  1285.2 628.3 %all-gather.73.cloned.1.call-start = ((), (), s32[]{:S(2)}) async-start(), calls=%async_computation.30 | async-start | bytes 22282240 | tf_op jit(solution)/shard_map/cond/branch_1_fun/all_gather | solution.py:351
  1309.7 123.2 %collective-permute-start.84 = (f32[2,256,1024]{2,1,0:T(8,128)}, f32[2,256,1024]{2,1,0:T(8,128)}, u32[]{:S(2)}, u32[]{:S(2)}) collective-permute-start(f32[2,256,1024]{2,1,0:T(8,128)} %dynamic-slice_bitcast_fusion.33), channel_id=1, source_target_pairs={{0,4},{1,5},{2,6},{3,7},{4,0},{5,1},{6,2},{7,3},{8,12},{9,13},{10,... | collective-permute-start | bytes 6291464 | tf_op jit(solution)/shard_map/cond/branch_1_fun/ppermute | solution.py:201
  1311.3 124.6 %collective-permute-start.86 = (f32[2,256,1024]{2,1,0:T(8,128)}, f32[2,256,1024]{2,1,0:T(8,128)}, u32[]{:S(2)}, u32[]{:S(2)}) collective-permute-start(f32[2,256,1024]{2,1,0:T(8,128)} %dynamic-slice_bitcast_fusion.32), channel_id=1, source_target_pairs={{0,8},{1,9},{2,10},{3,11},{4,12},{5,13},{6,14},{7,15},{8,0},{9,1},... | collective-permute-start | bytes 6291464 | tf_op jit(solution)/shard_map/cond/branch_1_fun/ppermute | solution.py:201
  1311.8 118.5 %collective-permute-start.85 = (f32[2,64,1024]{2,1,0:T(8,128)}, f32[2,64,1024]{2,1,0:T(8,128)}, u32[]{:S(2)}, u32[]{:S(2)}) collective-permute-start(f32[2,64,1024]{2,1,0:T(8,128)} %dynamic-slice_bitcast_fusion.49), channel_id=1, source_target_pairs={{0,4},{1,5},{2,6},{3,7},{4,0},{5,1},{6,2},{7,3},{8,12},{9,13},{10,... | collective-permute-start | bytes 1572872 | tf_op jit(solution)/shard_map/cond/branch_1_fun/ppermute | solution.py:201
  1312.5 119.2 %collective-permute-start.87 = (f32[2,64,1024]{2,1,0:T(8,128)}, f32[2,64,1024]{2,1,0:T(8,128)}, u32[]{:S(2)}, u32[]{:S(2)}) collective-permute-start(f32[2,64,1024]{2,1,0:T(8,128)} %dynamic-slice_bitcast_fusion.48), channel_id=1, source_target_pairs={{0,8},{1,9},{2,10},{3,11},{4,12},{5,13},{6,14},{7,15},{8,0},{9,1},... | collective-permute-start | bytes 1572872 | tf_op jit(solution)/shard_map/cond/branch_1_fun/ppermute | solution.py:201
  1315.2 173.2 %all-to-all-start.7 = ((f32[16,32,1024]{2,1,0:T(8,128)}), f32[16,32,1024]{2,1,0:T(8,128)}, u32[]{:S(2)}, u32[]{:S(2)}) async-start(f32[16,32,1024]{2,1,0:T(8,128)} %bitcast.1153), calls=%async_computation.7 | async-start | bytes 4194304 | tf_op jit(solution)/shard_map/cond/branch_1_fun/all_to_all | solution.py:299
  1318.4 687.4 %all-gather.63.cloned.1.call-start = ((), (), s32[]{:S(2)}) async-start(), calls=%async_computation.25 | async-start | bytes 22282240 | tf_op jit(solution)/shard_map/cond/branch_1_fun/all_gather | solution.py:351
  1491.0 607.1 %all-gather.71.cloned.1.call-start = ((), (), s32[]{:S(2)}) async-start(), calls=%async_computation.29 | async-start | bytes 22282240 | tf_op jit(solution)/shard_map/cond/branch_1_fun/all_gather | solution.py:351
  (145 other events, 3307.5 us)
Sparse Core Ops, SparseCore 0:
  608.3 66.7 all-gather.54
  781.8 53.5 all-gather.56
  956.9 60.1 all-gather.58
  1190.9 88.6 all-gather.60
  1281.6 155.0 all-gather.68
  1438.8 105.2 all-gather.76
  1546.3 90.0 all-gather.66
  1638.7 90.0 all-gather.74
  1731.1 90.0 all-gather.64
  1823.3 90.0 all-gather.72
  1915.7 90.0 all-gather.62
  2007.9 90.0 all-gather.70
